TPU v7x, 256 devices: a whole 4x4x8 slice. The times are simulated.
256 devices in a mesh: tok: 32 (over z, y), head: 4 (over x), grp: 2 (over core).
Axes of the slice: x: 4, y: 4, z: 8, core: 2. Of those that a mesh axis runs over, the one named last changes fastest.
Arguments:
- tokens: bfloat16 [16384, 4096], P('tok', ('head', 'grp')), may hold values from -6 to 6
- norm_gain: bfloat16 [4096], P(('head', 'grp')), may hold values from 1.2 to 9, as said below
- query_key_value_weight: bfloat16 [4096, 6144], P(None, ('head', 'grp')), may hold values from -0.09375 to 0.09375
- out_weight: bfloat16 [4096, 4096], P(('head', 'grp')), may hold values from -0.09375 to 0.09375
- doc_ids: int32 [16384], P('tok'), may hold values from 0 to 15, never falling along the last dimension, each value on 1 to 8192 neighbouring positions
Outputs:
- attended: bfloat16 [16384, 4096], P('tok', ('head', 'grp'))
Inputs may be any that keep to these rules, and one draw needn't show every extreme that they name: `norm_gain`: norm gains are positive. `doc_ids`: non-decreasing along the window; each document has 1 to 8192 tokens and one has exactly 8192.
All inputs are finite; a program needn't handle non-finite values.
Results may differ from a plain program's by a relative error of at most 0.019.
The roundings to bfloat16 on the way count: a program that leaves them out, or rounds other values in their place, can miss the bound.
Values may be sent and summed in bfloat16 or wider, within the bound.
No kernel may reach another device: no remote copies, remote signals or barrier semaphores. Data moves between devices by JAX's collectives and lax.ppermute only.
A program may use at most 128 MiB of HBM per device.

v0:
```python
import jax
import jax.numpy as jnp
from jax import lax
from jax.experimental import pallas as pl
from jax.experimental.pallas import tpu as pltpu
from jax.sharding import PartitionSpec as P


QUERY_HEADS = 32
KEY_VALUE_HEADS = 8
HEAD_SIZE = 128
GROUP = QUERY_HEADS // KEY_VALUE_HEADS
MODEL_WIDTH = 4096

T = 512
HALF = T // 2
PIECE = 512
Y, Z = 4, 8
LANES = 128
KV_ROWS = 2 * T
MSG_ROWS = KV_ROWS + 16

epsilon = 1e-05
theta = 500000.0
floor_score = -1e30
exponent_scale = HEAD_SIZE**-0.5 * 1.4426950408889634

bf16 = jnp.bfloat16
f32 = jnp.float32


def shift(x, axis, distance):
    n = lax.axis_size(axis)
    return lax.ppermute(x, axis, [(i, (i + distance) % n) for i in range(n)])


def shift_z(x):
    return lax.ppermute(
        x, "tok", [(z * Y + y, (z + 1) % Z * Y + y) for z in range(Z) for y in range(Y)]
    )


def shift_y(x, distance):
    return lax.ppermute(
        x, "tok", [(z * Y + y, z * Y + (y + distance) % Y) for z in range(Z) for y in range(Y)]
    )


def vmem(n):
    return [pl.BlockSpec(memory_space=pltpu.VMEM)] * n


def smem():
    return pl.BlockSpec(memory_space=pltpu.SMEM)


def params():
    return pltpu.CompilerParams(vmem_limit_bytes=56 << 20)


def project_kernel(
    fids, x0, p0, m0, q0, r0, x1, pm1, qr1, weight, cosine, sine, ids,
    queries, message, normed, held, mixed, sems,
):
    fetches = []
    for i in range(3):
        part = slice(i * 256, (i + 1) * 256)
        fetches.append(pltpu.make_async_copy(weight.at[:, part], held.at[i], sems.at[i]))
    for fetch in fetches:
        fetch.start()
    pieces = []
    rows = T + 16
    mine = ((x0, 0), (p0, 0), (m0, 0), (q0, 0), (r0, 0))
    theirs = ((x1, 0), (pm1, 0), (pm1, rows), (qr1, 0), (qr1, HALF))
    for *three, (q, top), (r, bottom) in (mine, theirs):
        for ref, base in three:
            pieces.append(((ref, base), (ref, base + HALF), (ref, base + T)))
        pieces.append(((q, top), (r, bottom), (r, bottom + HALF)))
    step_rows = 16
    for half in range(2):

        def step(i, _):
            row = pl.multiple_of(i * step_rows, step_rows)
            total = jnp.zeros((step_rows, PIECE), f32)
            for piece in pieces:
                ref, base = piece[half]
                v = ref[pl.ds(base + row, step_rows), :].astype(f32)
                total += v * v
            mean = jnp.sum(total, axis=1, keepdims=True) * (1.0 / MODEL_WIDTH)
            scale = lax.rsqrt(mean + epsilon)
            for k, piece in enumerate(pieces):
                ref, base = piece[half]
                gain_ref, gain_base = piece[2]
                gain = gain_ref[gain_base : gain_base + 16, :].astype(f32)
                v = ref[pl.ds(base + row, step_rows), :].astype(f32) * scale * gain
                column = pl.multiple_of(fids[k] * PIECE, PIECE)
                normed[pl.ds(half * HALF + row, step_rows), pl.ds(column, PIECE)] = v.astype(bf16)
            return 0

        lax.fori_loop(0, HALF // step_rows, step, 0)

    def columns(i, _):
        for j in range(3):
            pl.when(i == j)(fetches[j].wait)
        at = pl.multiple_of(i * 256, 256)
        mixed[:, pl.ds(at, 256)] = jnp.dot(normed[...], held[i], preferred_element_type=f32)
        return 0

    lax.fori_loop(0, (GROUP + 2) * HEAD_SIZE // 256, columns, 0)

    def rotated(h):
        v = mixed[:, h * HEAD_SIZE : (h + 1) * HEAD_SIZE]
        return v * cosine[...] + pltpu.roll(v, HEAD_SIZE // 2, 1) * sine[...]

    for h in range(GROUP):
        queries[h * HEAD_SIZE : (h + 1) * HEAD_SIZE, :] = rotated(h).astype(bf16).T
    message[0:T, :] = rotated(GROUP).astype(bf16)
    for j in range(T // LANES):
        v = mixed[j * LANES : (j + 1) * LANES, (GROUP + 1) * HEAD_SIZE :]
        message[T + j * LANES : T + (j + 1) * LANES, :] = v.astype(bf16).T
    message[KV_ROWS:MSG_ROWS, :] = ids[...]


def project(fids, pieces, weight, cosine, sine, ids):
    width = (GROUP + 2) * HEAD_SIZE
    return pl.pallas_call(
        project_kernel,
        out_shape=(
            jax.ShapeDtypeStruct((GROUP * HEAD_SIZE, T), bf16),
            jax.ShapeDtypeStruct((MSG_ROWS, LANES), bf16),
        ),
        in_specs=[smem()] + vmem(8) + [pl.BlockSpec(memory_space=pl.ANY)] + vmem(3),
        out_specs=tuple(vmem(2)),
        scratch_shapes=[
            pltpu.VMEM((T, MODEL_WIDTH), bf16),
            pltpu.VMEM((3, MODEL_WIDTH, 256), bf16),
            pltpu.VMEM((T, width), f32),
            pltpu.SemaphoreType.DMA((3,)),
        ],
        compiler_params=params(),
        cost_estimate=pl.CostEstimate(
            flops=2 * T * MODEL_WIDTH * width, transcendentals=0, bytes_accessed=12 << 20
        ),
        name="project",
    )(fids, *pieces, weight, cosine, sine, ids)


def attend_block(block, queries, highest, totals, accum, change, together):
    keys = block[0:T, :]
    values = jnp.concatenate(
        [block[T + j * LANES : T + (j + 1) * LANES, :] for j in range(T // LANES)], axis=1
    )

    def head(h):
        rows = pl.ds(pl.multiple_of(h * HEAD_SIZE, HEAD_SIZE), HEAD_SIZE)
        for at in range(0, T, LANES):
            part = slice(at, at + LANES)
            scores = jnp.dot(keys, queries[rows, part], preferred_element_type=f32)
            scores = change(scores, at)
            old = highest[h, :, part]
            new = jnp.maximum(old, jnp.max(scores, axis=0, keepdims=True))
            weights = jnp.exp2((scores - new) * exponent_scale)
            fade = jnp.exp2((old - new) * exponent_scale)
            highest[h, :, part] = new
            totals[h, :, part] = totals[h, :, part] * fade + jnp.sum(weights, axis=0, keepdims=True)
            accum[rows, part] = accum[rows, part] * fade + jnp.dot(
                values, weights.astype(bf16), preferred_element_type=f32
            )

    def heads(i, _):
        for j in range(together):
            head(i * together + j)
        return 0

    lax.fori_loop(0, GROUP // together, heads, 0)


def clear(highest, totals, accum):
    highest[...] = jnp.full(highest.shape, floor_score, f32)
    totals[...] = jnp.zeros(totals.shape, f32)
    accum[...] = jnp.zeros(accum.shape, f32)


def whole_of(ref):
    def copies(block, sems):
        return [pltpu.make_async_copy(ref.at[pl.ds(0, MSG_ROWS)], block, sems.at[0])]

    return copies


def pair_of(keys, base, values, value_base):
    rest = MSG_ROWS - T

    def copies(block, sems):
        return [
            pltpu.make_async_copy(keys.at[pl.ds(base, T)], block.at[pl.ds(0, T)], sems.at[0]),
            pltpu.make_async_copy(
                values.at[pl.ds(value_base, rest)], block.at[pl.ds(T, rest)], sems.at[1]
            ),
        ]

    return copies


def attend_earlier(info, which, sources, queries, blocks, bias, sems, fill, state):
    own, first_doc = info[0], info[1].astype(f32)

    def reached(j):
        index = info[3 + which[j]]
        return (index >= 0) & (index < own)

    def each(j, act):
        def run():
            for copy in sources[j](blocks.at[j], sems.at[j]):
                act(copy)

        return run

    for j in range(len(which)):
        pl.when(reached(j))(each(j, lambda copy: copy.start()))
    fill()

    def step(k, _):
        wanted = reached(0)
        for j in range(1, len(which)):
            wanted = jnp.where(k == j, reached(j), wanted)

        @pl.when(wanted)
        def _():
            for j in range(len(which)):
                pl.when(k == j)(each(j, lambda copy: copy.wait()))
            block = blocks.at[k]
            ids = block[KV_ROWS:MSG_ROWS, :].astype(f32)
            low = jnp.sum(jnp.where(ids < first_doc, 1.0, 0.0)).astype(jnp.int32)

            @pl.when(low < T)
            def _():
                key = lax.broadcasted_iota(jnp.int32, (T, LANES), 0)
                bias[...] = jnp.where(key < low, floor_score, 0.0)
                attend_block(block, queries, *state, lambda scores, at: scores + bias[...], 1 if len(which) == 3 and which[0] == 3 else TOGETHER)

        return 0

    lax.fori_loop(0, len(which), step, 0)


TOGETHER = 2
STATE = (
    jax.ShapeDtypeStruct((GROUP, 1, T), f32),
    jax.ShapeDtypeStruct((GROUP, 1, T), f32),
    jax.ShapeDtypeStruct((GROUP * HEAD_SIZE, T), f32),
)
BLOCK_FLOPS = 4 * GROUP * T * T * HEAD_SIZE


def earlier_scratch(n):
    return [
        pltpu.VMEM((n, MSG_ROWS, LANES), bf16),
        pltpu.VMEM((T, LANES), f32),
        pltpu.SemaphoreType.DMA((n, 2)),
    ]


def attend_first(queries, message, doc_rows, doc_columns):
    def kernel(message, queries, doc_rows, doc_columns, *state):
        clear(*state)

        def change(scores, at):
            key = lax.broadcasted_iota(jnp.int32, scores.shape, 0)
            query = lax.broadcasted_iota(jnp.int32, scores.shape, 1) + at
            same = doc_rows[...] == doc_columns[0:1, at : at + LANES]
            return jnp.where((key <= query) & same, scores, floor_score)

        attend_block(message, queries, *state, change, 1)

    return pl.pallas_call(
        kernel,
        out_shape=STATE,
        in_specs=vmem(4),
        out_specs=tuple(vmem(3)),
        compiler_params=params(),
        cost_estimate=pl.CostEstimate(
            flops=2 * BLOCK_FLOPS, transcendentals=GROUP * T * T, bytes_accessed=2 << 20
        ),
        name="attend_own",
    )(message, queries, doc_rows, doc_columns)


def attend_stage(info, queries, state, along, against, straight, between, which):
    n = 2 + (straight is not None)

    def kernel(info, queries, *refs):
        refs = list(refs)
        messages = [refs.pop(0) for _ in range(n)]
        old = [refs.pop(0) for _ in state]
        new = [refs.pop(0) for _ in range(3)]

        def fill():
            if old:
                for a, b in zip(old, new):
                    b[...] = a[...]
            else:
                clear(*new)

        sources = [whole_of(m) for m in messages]
        if between:
            sources.append(pair_of(messages[0], MSG_ROWS, messages[1], MSG_ROWS))
        attend_earlier(info, which, sources, queries, *refs, fill, new)

    messages = [along, against] + ([straight] if straight is not None else [])
    return pl.pallas_call(
        kernel,
        out_shape=STATE,
        in_specs=[smem()] + vmem(1) + [pl.BlockSpec(memory_space=pl.ANY)] * n + vmem(len(state)),
        out_specs=tuple(vmem(3)),
        scratch_shapes=earlier_scratch(len(which)),
        input_output_aliases={2 + n + i: i for i in range(len(state))},
        compiler_params=params(),
        cost_estimate=pl.CostEstimate(
            flops=2 * len(which) * BLOCK_FLOPS,
            transcendentals=len(which) * GROUP * T * T,
            bytes_accessed=3 << 20,
        ),
        name="attend_stage",
    )(info, queries, *messages, *state)


def fetch_columns(columns, first, count, weight, held, sems):
    fetches = []
    for k in range(count):
        at = pl.multiple_of(columns[first + k] * PIECE, PIECE)
        fetches.append(pltpu.make_async_copy(weight.at[:, pl.ds(at, PIECE)], held.at[k], sems.at[k]))
    for fetch in fetches:
        fetch.start()
    return fetches


def column_scratch(count):
    return [
        pltpu.VMEM((count, GROUP * HEAD_SIZE, PIECE), bf16),
        pltpu.SemaphoreType.DMA((count,)),
    ]


def finish(info, queries, own_state, state, keys, values, which, columns, weight):
    def kernel(
        info, columns, queries, keys, values, own_highest, own_totals, own_accum,
        old_highest, old_totals, old_accum, weight,
        heads, first, others, far, highest, totals, accum, blocks, bias, sems, held, held_sems,
    ):
        fetches = fetch_columns(columns, 0, 5, weight, held, held_sems)

        def fill():
            highest[...] = old_highest[...]
            totals[...] = old_totals[...]
            accum[...] = old_accum[...]

        attend_earlier(
            info, which, [pair_of(keys, 0, values, 0)], queries, blocks, bias, sems, fill,
            (highest, totals, accum),
        )
        query = lax.broadcasted_iota(jnp.int32, (1, T), 1)
        for h in range(GROUP):
            rows = slice(h * HEAD_SIZE, (h + 1) * HEAD_SIZE)
            used = (query < info[2]) & (totals[h] > 0.0)
            near, past = own_highest[h], highest[h]
            top = jnp.where(used, jnp.maximum(near, past), near)
            near = jnp.exp2((near - top) * exponent_scale)
            past = jnp.where(used, jnp.exp2((past - top) * exponent_scale), 0.0)
            total = own_totals[h] * near + totals[h] * past
            summed = own_accum[rows, :] * near + accum[rows, :] * past
            heads[:, rows] = (summed / total).astype(bf16).T

        def multiply(k, _):
            for j in range(5):
                pl.when(k == j)(fetches[j].wait)
            far[...] = jnp.dot(heads[...], held[k], preferred_element_type=f32)

            @pl.when(k == 0)
            def _():
                first[...] = far[...].astype(bf16)

            @pl.when((k > 0) & (k < 4))
            def _():
                others[jnp.clip(k - 1, 0, 2)] = far[...].astype(bf16)

            return 0

        lax.fori_loop(0, 5, multiply, 0)

    return pl.pallas_call(
        kernel,
        out_shape=(
            jax.ShapeDtypeStruct((T, GROUP * HEAD_SIZE), bf16),
            jax.ShapeDtypeStruct((T, PIECE), bf16),
            jax.ShapeDtypeStruct((3, T, PIECE), bf16),
            jax.ShapeDtypeStruct((T, PIECE), f32),
        ),
        in_specs=[smem(), smem()]
        + vmem(1)
        + [pl.BlockSpec(memory_space=pl.ANY)] * 2
        + vmem(6)
        + [pl.BlockSpec(memory_space=pl.ANY)],
        out_specs=tuple(vmem(4)),
        scratch_shapes=[
            pltpu.VMEM((GROUP, 1, T), f32),
            pltpu.VMEM((GROUP, 1, T), f32),
            pltpu.VMEM((GROUP * HEAD_SIZE, T), f32),
        ]
        + earlier_scratch(1)
        + column_scratch(5),
        compiler_params=params(),
        cost_estimate=pl.CostEstimate(
            flops=2 * T * T * MODEL_WIDTH, transcendentals=0, bytes_accessed=8 << 20
        ),
        name="finish",
    )(info, columns, queries, keys, values, *own_state, *state, weight)


def own_products(columns, heads, weight):
    def kernel(columns, heads, weight, out, held, sems):
        fetches = fetch_columns(columns, 5, 3, weight, held, sems)

        def multiply(k, _):
            for j in range(3):
                pl.when(k == j)(fetches[j].wait)
            out[k] = jnp.dot(heads[...], held[k], preferred_element_type=f32)
            return 0

        lax.fori_loop(0, 3, multiply, 0)

    return pl.pallas_call(
        kernel,
        out_shape=jax.ShapeDtypeStruct((3, T, PIECE), f32),
        in_specs=[smem()] + vmem(1) + [pl.BlockSpec(memory_space=pl.ANY)],
        out_specs=vmem(1)[0],
        scratch_shapes=column_scratch(3),
        compiler_params=params(),
        cost_estimate=pl.CostEstimate(
            flops=2 * T * T * MODEL_WIDTH // 2, transcendentals=0, bytes_accessed=6 << 20
        ),
        name="own_products",
    )(columns, heads, weight)


def body(tokens, norm_gain, query_key_value_weight, out_weight, doc_ids):
    shard = lax.axis_index("tok")
    chip = lax.axis_index("head")
    core = lax.axis_index("grp")
    row, column = shard // Y, shard % Y

    own = jnp.concatenate([tokens, jnp.broadcast_to(norm_gain[None, :], (16, PIECE))], axis=0)
    behind = shift(own, "head", 1)
    ahead = shift(own, "head", -1)
    across = shift(own, "grp", 1)
    chips = jnp.stack([chip, (chip - 1) % 4, (chip + 1) % 4, (chip + 2) % 4])
    fids = jnp.concatenate([chips * 2 + core, chips * 2 + 1 - core]).astype(jnp.int32)

    positions = shard * T + jnp.arange(T, dtype=jnp.int32)
    half = HEAD_SIZE // 2
    inverse = 1.0 / theta ** (jnp.arange(half, dtype=f32) * (2.0 / HEAD_SIZE))
    angles = positions.astype(f32)[:, None] * inverse[None, :]
    cosine, sine = jnp.cos(angles), jnp.sin(angles)
    cosine = jnp.concatenate([cosine, cosine], axis=1)
    sine = jnp.concatenate([-sine, sine], axis=1)
    ids = jnp.concatenate(
        [doc_ids.reshape(T // LANES, LANES), jnp.full((16 - T // LANES, LANES), 99, jnp.int32)]
    ).astype(bf16)
    doc_rows = jnp.broadcast_to(doc_ids.astype(f32)[:, None], (T, LANES))
    doc_columns = jnp.broadcast_to(doc_ids.astype(f32)[None, :], (8, T))

    blocks = [4 * (row - s) + (column + k) % Y for s in range(5) for k in range(4)]
    info = jnp.stack(
        [shard, doc_ids[0], jnp.sum((doc_ids == doc_ids[0]).astype(jnp.int32))] + blocks
    ).astype(jnp.int32)
    order = jnp.stack([(chip + 2) % 4, (chip + 1) % 4, (chip + 3) % 4, chip])
    columns = jnp.concatenate([order * 2 + 1 - core, order * 2 + core]).astype(jnp.int32)

    behind, ahead, across = lax.optimization_barrier((behind, ahead, across))
    top = shift(behind[:HALF], "head", 1)
    bottom = shift(ahead[HALF:], "head", -1)
    across_near = shift(jnp.concatenate([behind, ahead]), "grp", 1)
    top, bottom, fids, info, columns, cosine, sine, ids, doc_rows, doc_columns = (
        lax.optimization_barrier(
            (top, bottom, fids, info, columns, cosine, sine, ids, doc_rows, doc_columns)
        )
    )
    mine = [own, behind, ahead, top, bottom]
    across_far = shift(jnp.concatenate([top, bottom]), "grp", 1)
    theirs = [across, across_near, across_far]
    queries, message = project(fids, mine + theirs, query_key_value_weight, cosine, sine, ids)

    straight = message
    own_state = attend_first(queries, message, doc_rows, doc_columns)
    state = ()
    along, against = message, message
    for s in range(5):
        next_along = shift_y(along, 1)
        next_against = shift_y(against, -1)
        following = shift_z(straight) if s < 4 else None
        which = [4 * s + 3, 4 * s + 1]
        if s < 4:
            which.append(4 * (s + 1))
        if s > 0:
            which.append(4 * (s - 1) + 2)
        state = attend_stage(
            info, queries, state, next_along, next_against, following, s > 0, which
        )
        forward, backward = next_along[0:T], next_against[T:MSG_ROWS]
        if s < 4:
            straight = following
            along = jnp.concatenate([straight, forward], axis=0)
            against = jnp.concatenate([straight, backward], axis=0)
    keys = shift_y(forward, 1)
    values = shift_y(backward, -1)

    heads, first, others, products = finish(
        info, queries, own_state, state, keys, values, [4 * 4 + 2], columns, out_weight
    )
    first = shift(first, "grp", 1)
    others = shift(others, "grp", 1)
    own_three = own_products(columns, heads, out_weight)

    far = (products + first.astype(f32)).astype(bf16)
    far_up = shift(far[:HALF], "head", 1)
    far_down = shift(far[HALF:], "head", -1)
    products = own_three
    up_low = (products[0, HALF:] + others[0, HALF:].astype(f32)).astype(bf16)
    down_high = (products[1, :HALF] + others[1, :HALF].astype(f32)).astype(bf16)
    up_low = shift(up_low, "head", 1)
    down_high = shift(down_high, "head", -1)
    up_high = products[0, :HALF] + others[0, :HALF].astype(f32) + far_up.astype(f32)
    down_low = products[1, HALF:] + others[1, HALF:].astype(f32) + far_down.astype(f32)
    up_high = shift(up_high.astype(bf16), "head", 1)
    down_low = shift(down_low.astype(bf16), "head", -1)
    kept = products[2] + others[2].astype(f32)
    return jnp.concatenate(
        [
            kept[:HALF] + up_high.astype(f32) + down_high.astype(f32),
            kept[HALF:] + up_low.astype(f32) + down_low.astype(f32),
        ]
    ).astype(bf16)


def solution(mesh):
    return jax.shard_map(
        body,
        mesh=mesh,
        in_specs=(
            P("tok", ("head", "grp")),
            P(("head", "grp")),
            P(None, ("head", "grp")),
            P(("head", "grp"), None),
            P("tok"),
        ),
        out_specs=P("tok", ("head", "grp")),
        check_vma=False,
    )
```

profile of v0, /device:TPU:134, one launch (start us, length us, event | category | flops | bytes accessed | tf_op | source)
XLA Modules:
  0.0 170.2 jit_solution(12799285760331811571)
XLA Ops:
  0.0 0.7 broadcast_in_dim.6
  0.7 1.1 pad_maximum_fusion.1.x0
  1.8 0.6 collective-permute-start
  2.3 1.5 collective-permute-start.1
  3.9 1.2 slice.90
  5.2 2.1 %fusion.18 = (f32[512]{0:T(512)S(1)}, s32[]{:T(128)}, bf16[4,128]{1,0:T(4,128)(2,1)S(1)}) fusion(s32[512]{0:T(512)} %param.9, s32[]{:T(128)} %bitcast.5), kind=kLoop, calls=%fused_computation.54 | loop fusion | flops 2559 | bytes 5128 | tf_op jit(solution)/shard_map/convert_element_type | solution.py:469
  7.3 1.0 fusion.16
  8.3 7.5 %collective-permute-done.p0 = bf16[528,512]{1,0:T(8,128)(2,1)S(1)} collective-permute-done((bf16[528,512]{1,0:T(8,128)(2,1)S(1)}, bf16[528,512]{1,0:T(8,128)(2,1)S(1)}, u32[]{:S(2)}, u32[]{:S(2)}) %collective-permute-start) | collective-permute-done | bytes 540704 | tf_op jit(solution)/shard_map/ppermute | solution.py:34
  15.9 1.4 collective-permute-done.1.m0
  17.5 0.7 slice.89
  18.2 0.7 slice.88
  18.9 0.3 collective-permute-start.4
  19.3 2.9 %collective-permute-start.3 = (bf16[256,512]{1,0:T(8,128)(2,1)}, bf16[256,512]{1,0:T(8,128)(2,1)S(1)}, u32[]{:S(2)}, u32[]{:S(2)}) collective-permute-start(bf16[256,512]{1,0:T(8,128)(2,1)} %slice.88), channel_id=1, source_target_pairs={{0,2},{2,4},{4,6},{6,0},{1,3},{3,5},{5,7},{7,1},{8,10},{10,12},{12... | collective-permute-start | bytes 786440 | tf_op jit(solution)/shard_map/ppermute | solution.py:34
  22.2 0.7 pad_add_fusion.fids
  22.8 0.6 concatenate.57.ids
  23.4 1.8 %stack.120.info = s32[23]{0:T(128)} concatenate(s32[1]{0:T(128)} %bitcast.4, s32[1]{0:T(128)} %slice.90, s32[1]{0:T(128)} %bitcast.6, s32[1]{0:T(128)} %bitcast.7, s32[1]{0:T(128)} %bitcast.8, s32[1]{0:T(128)} %bitcast.9, s32[1]{0:T(128)} %bitcast.10, s32[1]{0:T(128)} %bitcast.11, s32[1]{0:T(128)} %bitcast.12, s32[1]{0:T(128)} %bitcast.13, s32[1]{0:T(128)} %bitcast.14, ...), dimensions={0} | concatenate | bytes 184 | tf_op jit(solution)/shard_map/stack | solution.py:473
  25.3 0.6 pad_add_fusion.1.columns
  25.9 1.0 pad_maximum_fusion.12
  26.9 1.5 collective-permute-done.3.q0
  28.4 1.0 collective-permute-done.4.r0
  29.4 0.8 broadcast_in_dim.7.doc_rows
  30.2 0.6 broadcast_in_dim.8.doc_columns
  31.0 1.9 %collective-permute-done.6.qr1 = bf16[528,512]{1,0:T(8,128)(2,1)S(1)} collective-permute-done((bf16[528,512]{1,0:T(8,128)(2,1)S(1)}, bf16[528,512]{1,0:T(8,128)(2,1)S(1)}, u32[]{:S(2)}, u32[]{:S(2)}) %collective-permute-start.6) | collective-permute-done | bytes 540704 | tf_op jit(solution)/shard_map/ppermute | solution.py:34
  32.9 0.8 copy-done.19
  33.7 12.0 %project.1 = (bf16[512,512]{1,0:T(8,128)(2,1)}, bf16[1040,128]{1,0:T(8,128)(2,1)}) custom-call(s32[8]{0:T(128)} %pad_add_fusion.fids, bf16[528,512]{1,0:T(8,128)(2,1)} %copy-done.6, bf16[528,512]{1,0:T(8,128)(2,1)} %copy-done.1, bf16[528,512]{1,0:T(8,128)(2,1)} %copy-done, bf16[256,512]{1,0:T(8,128)(2,1)} %copy-done.8, bf16[272,512]{1,0:T(8,128)(2,1)} %copy-done.7, ...), custom_call_target="tpu_custom_call" | custom-call | flops 3221225472 | bytes 12582912 | tf_op jit(solution)/shard_map/project/pallas_call | solution.py:126
  45.7 1.7 collective-permute-start.11
  47.3 1.0 collective-permute-start.7
  48.4 1.7 collective-permute-start.17
  50.0 5.0 %attend_own.1 = (f32[4,1,512]{2,1,0:T(1,128)}, f32[4,1,512]{2,1,0:T(1,128)}, f32[512,512]{1,0:T(8,128)}) custom-call(bf16[1040,128]{1,0:T(8,128)(2,1)} %get-tuple-element.54.message, bf16[512,512]{1,0:T(8,128)(2,1)} %get-tuple-element.53.queries, f32[512,128]{1,0:T(8,128)} %broadcast_in_dim.7.doc_rows, f32[8,512]{1,0:T(8,128)} %broadcast_in_dim.8.doc_columns), custom_call_target="tpu_custom_call" | custom-call | flops 1073741824 | bytes 2097152 | tf_op jit(solution)/shard_map/attend_own/pallas_call | solution.py:276
  55.0 0.7 collective-permute-done.11.refs_0_
  55.7 1.2 collective-permute-done.7.refs_2_
  56.9 1.8 %collective-permute-start.12 = (bf16[1552,128]{1,0:T(8,128)(2,1)S(1)}, bf16[1552,128]{1,0:T(8,128)(2,1)S(1)}, u32[]{:S(2)}, u32[]{:S(2)}) collective-permute-start(bf16[1552,128]{1,0:T(8,128)(2,1)S(1)} %pad_maximum_fusion.8), channel_id=1, source_target_pairs={{0,8},{8,16},{16,24},{24,0},{32,40},{40,48},{48,56},{56,32},{64,72... | collective-permute-start | bytes 1191944 | tf_op jit(solution)/shard_map/ppermute | solution.py:44
  58.8 1.7 %collective-permute-start.18 = (bf16[1568,128]{1,0:T(8,128)(2,1)S(1)}, bf16[1568,128]{1,0:T(8,128)(2,1)S(1)}, u32[]{:S(2)}, u32[]{:S(2)}) collective-permute-start(bf16[1568,128]{1,0:T(8,128)(2,1)S(1)} %pad_maximum_fusion.4), channel_id=1, source_target_pairs={{0,24},{8,0},{16,8},{24,16},{32,56},{40,32},{48,40},{56,48},{64,88... | collective-permute-start | bytes 1204232 | tf_op jit(solution)/shard_map/ppermute | solution.py:44
  60.6 5.9 %attend_stage.5 = (f32[4,1,512]{2,1,0:T(1,128)}, f32[4,1,512]{2,1,0:T(1,128)}, f32[512,512]{1,0:T(8,128)}) custom-call(s32[23]{0:T(128)} %stack.120.info, bf16[512,512]{1,0:T(8,128)(2,1)} %get-tuple-element.53.queries, bf16[1040,128]{1,0:T(8,128)(2,1)} %copy-done.10, bf16[1040,128]{1,0:T(8,128)(2,1)} %copy-done.9, bf16[1040,128]{1,0:T(8,128)(2,1)} %copy-done.5), custom_call_target="tpu_custom_call" | custom-call | flops 3221225472 | bytes 3145728 | tf_op jit(solution)/shard_map/attend_stage/pallas_call | solution.py:311
  66.6 2.0 %collective-permute-done.8.refs_2_ = bf16[1040,128]{1,0:T(8,128)(2,1)S(1)} collective-permute-done((bf16[1040,128]{1,0:T(8,128)(2,1)S(1)}, bf16[1040,128]{1,0:T(8,128)(2,1)S(1)}, u32[]{:S(2)}, u32[]{:S(2)}) %collective-permute-start.8) | collective-permute-done | bytes 266272 | tf_op jit(solution)/shard_map/ppermute | solution.py:38
  68.6 1.5 collective-permute-start.13
  70.2 3.2 %collective-permute-start.19 = (bf16[1568,128]{1,0:T(8,128)(2,1)S(1)}, bf16[1568,128]{1,0:T(8,128)(2,1)S(1)}, u32[]{:S(2)}, u32[]{:S(2)}) collective-permute-start(bf16[1568,128]{1,0:T(8,128)(2,1)S(1)} %pad_maximum_fusion.5), channel_id=1, source_target_pairs={{0,24},{8,0},{16,8},{24,16},{32,56},{40,32},{48,40},{56,48},{64,88... | collective-permute-start | bytes 1204232 | tf_op jit(solution)/shard_map/ppermute | solution.py:44
  73.4 10.2 %attend_stage.6 = (f32[4,1,512]{2,1,0:T(1,128)}, f32[4,1,512]{2,1,0:T(1,128)}, f32[512,512]{1,0:T(8,128)}) custom-call(s32[23]{0:T(128)} %stack.120.info, bf16[512,512]{1,0:T(8,128)(2,1)} %get-tuple-element.53.queries, bf16[1552,128]{1,0:T(8,128)(2,1)} %copy-done.15, ...), custom_call_target="tpu_custom_call", output_to_operand_aliasing={{0}: (5, {}), {1}: (6, {}), {2}: (7, {})} | custom-call | flops 4294967296 | bytes 3145728 | tf_op jit(solution)/shard_map/attend_stage/pallas_call | solution.py:311
  83.9 4.3 %collective-permute-start.20 = (bf16[1568,128]{1,0:T(8,128)(2,1)S(1)}, bf16[1568,128]{1,0:T(8,128)(2,1)S(1)}, u32[]{:S(2)}, u32[]{:S(2)}) collective-permute-start(bf16[1568,128]{1,0:T(8,128)(2,1)S(1)} %pad_maximum_fusion.6), channel_id=1, source_target_pairs={{0,24},{8,0},{16,8},{24,16},{32,56},{40,32},{48,40},{56,48},{64,88... | collective-permute-start | bytes 1204232 | tf_op jit(solution)/shard_map/ppermute | solution.py:44
  88.2 12.4 %attend_stage.7 = (f32[4,1,512]{2,1,0:T(1,128)}, f32[4,1,512]{2,1,0:T(1,128)}, f32[512,512]{1,0:T(8,128)}) custom-call(s32[23]{0:T(128)} %stack.120.info, bf16[512,512]{1,0:T(8,128)(2,1)} %get-tuple-element.53.queries, bf16[1552,128]{1,0:T(8,128)(2,1)} %copy-done.16, ...), custom_call_target="tpu_custom_call", output_to_operand_aliasing={{0}: (5, {}), {1}: (6, {}), {2}: (7, {})} | custom-call | flops 4294967296 | bytes 3145728 | tf_op jit(solution)/shard_map/attend_stage/pallas_call | solution.py:311
  100.8 0.7 collective-permute-start.15
  101.5 3.0 %collective-permute-start.21 = (bf16[1568,128]{1,0:T(8,128)(2,1)S(1)}, bf16[1568,128]{1,0:T(8,128)(2,1)S(1)}, u32[]{:S(2)}, u32[]{:S(2)}) collective-permute-start(bf16[1568,128]{1,0:T(8,128)(2,1)S(1)} %pad_maximum_fusion.7), channel_id=1, source_target_pairs={{0,24},{8,0},{16,8},{24,16},{32,56},{40,32},{48,40},{56,48},{64,88... | collective-permute-start | bytes 1204232 | tf_op jit(solution)/shard_map/ppermute | solution.py:44
  104.4 10.3 %attend_stage.8 = (f32[4,1,512]{2,1,0:T(1,128)}, f32[4,1,512]{2,1,0:T(1,128)}, f32[512,512]{1,0:T(8,128)}) custom-call(s32[23]{0:T(128)} %stack.120.info, bf16[512,512]{1,0:T(8,128)(2,1)} %get-tuple-element.53.queries, bf16[1552,128]{1,0:T(8,128)(2,1)} %copy-done.17, ...), custom_call_target="tpu_custom_call", output_to_operand_aliasing={{0}: (5, {}), {1}: (6, {}), {2}: (7, {})} | custom-call | flops 4294967296 | bytes 3145728 | tf_op jit(solution)/shard_map/attend_stage/pallas_call | solution.py:311
  115.0 3.3 %collective-permute-start.22 = (bf16[528,128]{1,0:T(8,128)(2,1)S(1)}, bf16[528,128]{1,0:T(8,128)(2,1)S(1)}, u32[]{:S(2)}, u32[]{:S(2)}) collective-permute-start(bf16[528,128]{1,0:T(8,128)(2,1)S(1)} %slice.126), channel_id=1, source_target_pairs={{0,24},{8,0},{16,8},{24,16},{32,56},{40,32},{48,40},{56,48},{64,88... | collective-permute-start | bytes 405512 | tf_op jit(solution)/shard_map/ppermute | solution.py:44
  118.2 8.1 %attend_stage.9 = (f32[4,1,512]{2,1,0:T(1,128)}, f32[4,1,512]{2,1,0:T(1,128)}, f32[512,512]{1,0:T(8,128)}) custom-call(s32[23]{0:T(128)} %stack.120.info, bf16[512,512]{1,0:T(8,128)(2,1)} %get-tuple-element.53.queries, bf16[1552,128]{1,0:T(8,128)(2,1)} %copy-done.18, ...), custom_call_target="tpu_custom_call", output_to_operand_aliasing={{0}: (4, {}), {1}: (5, {}), {2}: (6, {})} | custom-call | flops 3221225472 | bytes 3145728 | tf_op jit(solution)/shard_map/attend_stage/pallas_call | solution.py:311
  126.4 0.6 copy-done.21
  127.1 8.4 %finish.1 = (bf16[512,512]{1,0:T(8,128)(2,1)}, bf16[512,512]{1,0:T(8,128)(2,1)}, bf16[3,512,512]{2,1,0:T(8,128)(2,1)}, f32[512,512]{1,0:T(8,128)}) custom-call(s32[23]{0:T(128)} %stack.120.info, s32[8]{0:T(128)} %pad_add_fusion.1.columns, bf16[512,512]{1,0:T(8,128)(2,1)} %get-tuple-element.53.queries, bf16[512,128]{1,0:T(8,128)(2,1)} %copy-done.21, ...), custom_call_target="tpu_custom_call" | custom-call | flops 2147483648 | bytes 8388608 | tf_op jit(solution)/shard_map/finish/pallas_call | solution.py:391
  135.6 0.5 collective-permute-start.24
  136.1 3.9 %collective-permute-done.24 = bf16[512,512]{1,0:T(8,128)(2,1)S(1)} collective-permute-done((bf16[512,512]{1,0:T(8,128)(2,1)}, bf16[512,512]{1,0:T(8,128)(2,1)S(1)}, u32[]{:S(2)}, u32[]{:S(2)}) %collective-permute-start.24) | collective-permute-done | bytes 524320 | tf_op jit(solution)/shard_map/ppermute | solution.py:34
  139.9 1.4 add_convert_fusion
  141.4 2.7 %collective-permute-start.25 = (bf16[256,512]{1,0:T(8,128)(2,1)S(1)}, bf16[256,512]{1,0:T(8,128)(2,1)S(1)}, u32[]{:S(2)}, u32[]{:S(2)}) collective-permute-start(bf16[256,512]{1,0:T(8,128)(2,1)S(1)} %get-tuple-element.89), channel_id=1, source_target_pairs={{0,2},{2,4},{4,6},{6,0},{1,3},{3,5},{5,7},{7,1},{8,10},{10,12},{12... | collective-permute-start | bytes 786440 | tf_op jit(solution)/shard_map/ppermute | solution.py:34
  144.1 5.1 %own_products.1 = f32[3,512,512]{2,1,0:T(8,128)} custom-call(s32[8]{0:T(128)} %pad_add_fusion.1.columns, bf16[512,512]{1,0:T(8,128)(2,1)} %get-tuple-element.75.heads, bf16[512,4096]{1,0:T(8,128)(2,1)} %weight.5), custom_call_target="tpu_custom_call" | custom-call | flops 1073741824 | bytes 6291456 | tf_op jit(solution)/shard_map/own_products/pallas_call | solution.py:432
  149.2 0.8 collective-permute-done.25
  150.0 3.4 %collective-permute-done.29 = bf16[256,512]{1,0:T(8,128)(2,1)S(1)} collective-permute-done((bf16[256,512]{1,0:T(8,128)(2,1)S(1)}, bf16[256,512]{1,0:T(8,128)(2,1)S(1)}, u32[]{:S(2)}, u32[]{:S(2)}) %collective-permute-start.29) | collective-permute-done | bytes 262176 | tf_op jit(solution)/shard_map/ppermute | solution.py:34
  153.4 1.4 fusion.10
  154.8 0.4 collective-permute-start.26
  155.1 1.7 %collective-permute-start.30 = (bf16[256,512]{1,0:T(8,128)(2,1)S(1)}, bf16[256,512]{1,0:T(8,128)(2,1)S(1)}, u32[]{:S(2)}, u32[]{:S(2)}) collective-permute-start(bf16[256,512]{1,0:T(8,128)(2,1)S(1)} %get-tuple-element.84), channel_id=1, source_target_pairs={{0,6},{2,0},{4,2},{6,4},{1,7},{3,1},{5,3},{7,5},{8,14},{10,8},{12,... | collective-permute-start | bytes 786440 | tf_op jit(solution)/shard_map/ppermute | solution.py:34
  156.9 1.4 fusion.14
  158.3 3.2 %collective-permute-start.28 = (bf16[256,512]{1,0:T(8,128)(2,1)S(1)}, bf16[256,512]{1,0:T(8,128)(2,1)S(1)}, u32[]{:S(2)}, u32[]{:S(2)}) collective-permute-start(bf16[256,512]{1,0:T(8,128)(2,1)S(1)} %get-tuple-element.86), channel_id=1, source_target_pairs={{0,2},{2,4},{4,6},{6,0},{1,3},{3,5},{5,7},{7,1},{8,10},{10,12},{12... | collective-permute-start | bytes 786440 | tf_op jit(solution)/shard_map/ppermute | solution.py:34
  161.6 1.4 slice_add_fusion
  163.0 1.1 collective-permute-done.26
  164.0 1.5 collective-permute-done.30
  165.5 3.7 %collective-permute-done.27 = bf16[256,512]{1,0:T(8,128)(2,1)S(1)} collective-permute-done((bf16[256,512]{1,0:T(8,128)(2,1)S(1)}, bf16[256,512]{1,0:T(8,128)(2,1)S(1)}, u32[]{:S(2)}, u32[]{:S(2)}) %collective-permute-start.27) | collective-permute-done | bytes 262176 | tf_op jit(solution)/shard_map/ppermute | solution.py:34
  169.4 0.8 pad_maximum_fusion.3
  (97 shorter events, 1.6 us)
Async XLA Ops:
  1.8 16.4 %copy-start.6 = (bf16[528,512]{1,0:T(8,128)(2,1)}, bf16[528,512]{1,0:T(8,128)(2,1)S(1)}, u32[]{:S(2)}) copy-start(bf16[528,512]{1,0:T(8,128)(2,1)S(1)} %pad_maximum_fusion.1.x0) | copy-start | bytes 1622020
  1.8 14.1 %collective-permute-start = (bf16[528,512]{1,0:T(8,128)(2,1)S(1)}, bf16[528,512]{1,0:T(8,128)(2,1)S(1)}, u32[]{:S(2)}, u32[]{:S(2)}) collective-permute-start(bf16[528,512]{1,0:T(8,128)(2,1)S(1)} %pad_maximum_fusion.1.x0), channel_id=1, source_target_pairs={{0,2},{2,4},{4,6},{6,0},{1,3},{3,5},{5,7},{7,1},{8,10},{10,12},{12... | collective-permute-start | bytes 1622024 | tf_op jit(solution)/shard_map/ppermute | solution.py:34
  2.3 14.9 %collective-permute-start.1 = (bf16[528,512]{1,0:T(8,128)(2,1)S(1)}, bf16[528,512]{1,0:T(8,128)(2,1)S(1)}, u32[]{:S(2)}, u32[]{:S(2)}) collective-permute-start(bf16[528,512]{1,0:T(8,128)(2,1)S(1)} %pad_maximum_fusion.1.x0), channel_id=1, source_target_pairs={{0,6},{2,0},{4,2},{6,4},{1,7},{3,1},{5,3},{7,5},{8,14},{10,8},{12,... | collective-permute-start | bytes 1622024 | tf_op jit(solution)/shard_map/ppermute | solution.py:34
  3.9 13.4 %collective-permute-start.2 = (bf16[528,512]{1,0:T(8,128)(2,1)S(1)}, bf16[528,512]{1,0:T(8,128)(2,1)}, u32[]{:S(2)}, u32[]{:S(2)}) collective-permute-start(bf16[528,512]{1,0:T(8,128)(2,1)S(1)} %pad_maximum_fusion.1.x0), channel_id=1, source_target_pairs={{0,1},{1,0},{2,3},{3,2},{4,5},{5,4},{6,7},{7,6},{8,9},{9,8},{10,11... | collective-permute-start | bytes 1622024 | tf_op jit(solution)/shard_map/ppermute | solution.py:34
  15.9 3.1 %copy-start.1 = (bf16[528,512]{1,0:T(8,128)(2,1)}, bf16[528,512]{1,0:T(8,128)(2,1)S(1)}, u32[]{:S(2)}) copy-start(bf16[528,512]{1,0:T(8,128)(2,1)S(1)} %collective-permute-done.p0) | copy-start | bytes 1622020
  17.3 1.6 copy-start
  17.4 15.6 %collective-permute-start.5 = (bf16[1056,512]{1,0:T(8,128)(2,1)S(1)}, bf16[1056,512]{1,0:T(8,128)(2,1)}, u32[]{:S(2)}, u32[]{:S(2)}) collective-permute-start(bf16[1056,512]{1,0:T(8,128)(2,1)S(1)} %pad_maximum_fusion), channel_id=1, source_target_pairs={{0,1},{1,0},{2,3},{3,2},{4,5},{5,4},{6,7},{7,6},{8,9},{9,8},{10,11... | collective-permute-start | bytes 3244040 | tf_op jit(solution)/shard_map/ppermute | solution.py:34
  18.9 10.5 %collective-permute-start.4 = (bf16[272,512]{1,0:T(8,128)(2,1)}, bf16[272,512]{1,0:T(8,128)(2,1)S(1)}, u32[]{:S(2)}, u32[]{:S(2)}) collective-permute-start(bf16[272,512]{1,0:T(8,128)(2,1)} %slice.89), channel_id=1, source_target_pairs={{0,6},{2,0},{4,2},{6,4},{1,7},{3,1},{5,3},{7,5},{8,14},{10,8},{12,... | collective-permute-start | bytes 835592 | tf_op jit(solution)/shard_map/ppermute | solution.py:34
  19.3 9.2 %collective-permute-start.3 = (bf16[256,512]{1,0:T(8,128)(2,1)}, bf16[256,512]{1,0:T(8,128)(2,1)S(1)}, u32[]{:S(2)}, u32[]{:S(2)}) collective-permute-start(bf16[256,512]{1,0:T(8,128)(2,1)} %slice.88), channel_id=1, source_target_pairs={{0,2},{2,4},{4,6},{6,0},{1,3},{3,5},{5,7},{7,1},{8,10},{10,12},{12... | collective-permute-start | bytes 786440 | tf_op jit(solution)/shard_map/ppermute | solution.py:34
  28.4 4.5 %copy-start.8 = (bf16[256,512]{1,0:T(8,128)(2,1)}, bf16[256,512]{1,0:T(8,128)(2,1)S(1)}, u32[]{:S(2)}) copy-start(bf16[256,512]{1,0:T(8,128)(2,1)S(1)} %collective-permute-done.3.q0) | copy-start | bytes 786436
  29.4 3.5 %copy-start.7 = (bf16[272,512]{1,0:T(8,128)(2,1)}, bf16[272,512]{1,0:T(8,128)(2,1)S(1)}, u32[]{:S(2)}) copy-start(bf16[272,512]{1,0:T(8,128)(2,1)S(1)} %collective-permute-done.4.r0) | copy-start | bytes 835588
  30.9 2.0 %collective-permute-start.6 = (bf16[528,512]{1,0:T(8,128)(2,1)S(1)}, bf16[528,512]{1,0:T(8,128)(2,1)S(1)}, u32[]{:S(2)}, u32[]{:S(2)}) collective-permute-start(bf16[528,512]{1,0:T(8,128)(2,1)S(1)} %pad_maximum_fusion.2), channel_id=1, source_target_pairs={{0,1},{1,0},{2,3},{3,2},{4,5},{5,4},{6,7},{7,6},{8,9},{9,8},{10,11... | collective-permute-start | bytes 1622024 | tf_op jit(solution)/shard_map/ppermute | solution.py:34
  32.9 0.8 copy-start.19
  45.7 10.0 %collective-permute-start.11 = (bf16[1040,128]{1,0:T(8,128)(2,1)}, bf16[1040,128]{1,0:T(8,128)(2,1)S(1)}, u32[]{:S(2)}, u32[]{:S(2)}) collective-permute-start(bf16[1040,128]{1,0:T(8,128)(2,1)} %get-tuple-element.54.message), channel_id=1, source_target_pairs={{0,8},{8,16},{16,24},{24,0},{32,40},{40,48},{48,56},{56,32},{64,72... | collective-permute-start | bytes 798728 | tf_op jit(solution)/shard_map/ppermute | solution.py:44
  47.3 9.6 %collective-permute-start.7 = (bf16[1040,128]{1,0:T(8,128)(2,1)}, bf16[1040,128]{1,0:T(8,128)(2,1)S(1)}, u32[]{:S(2)}, u32[]{:S(2)}) collective-permute-start(bf16[1040,128]{1,0:T(8,128)(2,1)} %get-tuple-element.54.message), channel_id=1, source_target_pairs={{0,32},{8,40},{16,48},{24,56},{32,64},{40,72},{48,80},{56,88},{64,... | collective-permute-start | bytes 798728 | tf_op jit(solution)/shard_map/ppermute | solution.py:38
  48.4 10.4 %collective-permute-start.17 = (bf16[1040,128]{1,0:T(8,128)(2,1)}, bf16[1040,128]{1,0:T(8,128)(2,1)S(1)}, u32[]{:S(2)}, u32[]{:S(2)}) collective-permute-start(bf16[1040,128]{1,0:T(8,128)(2,1)} %get-tuple-element.54.message), channel_id=1, source_target_pairs={{0,24},{8,0},{16,8},{24,16},{32,56},{40,32},{48,40},{56,48},{64,88... | collective-permute-start | bytes 798728 | tf_op jit(solution)/shard_map/ppermute | solution.py:44
  55.7 4.9 %copy-start.10 = (bf16[1040,128]{1,0:T(8,128)(2,1)}, bf16[1040,128]{1,0:T(8,128)(2,1)S(1)}, u32[]{:S(2)}) copy-start(bf16[1040,128]{1,0:T(8,128)(2,1)S(1)} %collective-permute-done.11.refs_0_) | copy-start | bytes 798724
  56.9 3.7 %copy-start.5 = (bf16[1040,128]{1,0:T(8,128)(2,1)}, bf16[1040,128]{1,0:T(8,128)(2,1)S(1)}, u32[]{:S(2)}) copy-start(bf16[1040,128]{1,0:T(8,128)(2,1)S(1)} %collective-permute-done.7.refs_2_) | copy-start | bytes 798724
  56.9 11.6 %collective-permute-start.12 = (bf16[1552,128]{1,0:T(8,128)(2,1)S(1)}, bf16[1552,128]{1,0:T(8,128)(2,1)S(1)}, u32[]{:S(2)}, u32[]{:S(2)}) collective-permute-start(bf16[1552,128]{1,0:T(8,128)(2,1)S(1)} %pad_maximum_fusion.8), channel_id=1, source_target_pairs={{0,8},{8,16},{16,24},{24,0},{32,40},{40,48},{48,56},{56,32},{64,72... | collective-permute-start | bytes 1191944 | tf_op jit(solution)/shard_map/ppermute | solution.py:44
  58.8 1.8 %copy-start.9 = (bf16[1040,128]{1,0:T(8,128)(2,1)}, bf16[1040,128]{1,0:T(8,128)(2,1)S(1)}, u32[]{:S(2)}) copy-start(bf16[1040,128]{1,0:T(8,128)(2,1)S(1)} %collective-permute-done.17.refs_1_) | copy-start | bytes 798724
  58.8 11.3 %collective-permute-start.18 = (bf16[1568,128]{1,0:T(8,128)(2,1)S(1)}, bf16[1568,128]{1,0:T(8,128)(2,1)S(1)}, u32[]{:S(2)}, u32[]{:S(2)}) collective-permute-start(bf16[1568,128]{1,0:T(8,128)(2,1)S(1)} %pad_maximum_fusion.4), channel_id=1, source_target_pairs={{0,24},{8,0},{16,8},{24,16},{32,56},{40,32},{48,40},{56,48},{64,88... | collective-permute-start | bytes 1204232 | tf_op jit(solution)/shard_map/ppermute | solution.py:44
  60.6 8.0 %collective-permute-start.8 = (bf16[1040,128]{1,0:T(8,128)(2,1)S(1)}, bf16[1040,128]{1,0:T(8,128)(2,1)S(1)}, u32[]{:S(2)}, u32[]{:S(2)}) collective-permute-start(bf16[1040,128]{1,0:T(8,128)(2,1)S(1)} %collective-permute-done.7.refs_2_), channel_id=1, source_target_pairs={{0,32},{8,40},{16,48},{24,56},{32,64},{40,72},{48,80},{56,88},{64,... | collective-permute-start | bytes 798728 | tf_op jit(solution)/shard_map/ppermute | solution.py:38
  68.5 4.8 %copy-start.4 = (bf16[1040,128]{1,0:T(8,128)(2,1)}, bf16[1040,128]{1,0:T(8,128)(2,1)S(1)}, u32[]{:S(2)}) copy-start(bf16[1040,128]{1,0:T(8,128)(2,1)S(1)} %collective-permute-done.8.refs_2_) | copy-start | bytes 798724
  68.5 15.1 %collective-permute-start.9 = (bf16[1040,128]{1,0:T(8,128)(2,1)S(1)}, bf16[1040,128]{1,0:T(8,128)(2,1)S(1)}, u32[]{:S(2)}, u32[]{:S(2)}) collective-permute-start(bf16[1040,128]{1,0:T(8,128)(2,1)S(1)} %collective-permute-done.8.refs_2_), channel_id=1, source_target_pairs={{0,32},{8,40},{16,48},{24,56},{32,64},{40,72},{48,80},{56,88},{64,... | collective-permute-start | bytes 798728 | tf_op jit(solution)/shard_map/ppermute | solution.py:38
  68.5 4.8 %copy-start.15 = (bf16[1552,128]{1,0:T(8,128)(2,1)}, bf16[1552,128]{1,0:T(8,128)(2,1)S(1)}, u32[]{:S(2)}) copy-start(bf16[1552,128]{1,0:T(8,128)(2,1)S(1)} %collective-permute-done.12.refs_0_) | copy-start | bytes 1191940
  68.6 15.1 %collective-permute-start.13 = (bf16[1552,128]{1,0:T(8,128)(2,1)S(1)}, bf16[1552,128]{1,0:T(8,128)(2,1)S(1)}, u32[]{:S(2)}, u32[]{:S(2)}) collective-permute-start(bf16[1552,128]{1,0:T(8,128)(2,1)S(1)} %pad_maximum_fusion.9), channel_id=1, source_target_pairs={{0,8},{8,16},{16,24},{24,0},{32,40},{40,48},{48,56},{56,32},{64,72... | collective-permute-start | bytes 1191944 | tf_op jit(solution)/shard_map/ppermute | solution.py:44
  70.1 3.3 %copy-start.11 = (bf16[1568,128]{1,0:T(8,128)(2,1)}, bf16[1568,128]{1,0:T(8,128)(2,1)S(1)}, u32[]{:S(2)}) copy-start(bf16[1568,128]{1,0:T(8,128)(2,1)S(1)} %collective-permute-done.18.refs_1_) | copy-start | bytes 1204228
  70.2 13.7 %collective-permute-start.19 = (bf16[1568,128]{1,0:T(8,128)(2,1)S(1)}, bf16[1568,128]{1,0:T(8,128)(2,1)S(1)}, u32[]{:S(2)}, u32[]{:S(2)}) collective-permute-start(bf16[1568,128]{1,0:T(8,128)(2,1)S(1)} %pad_maximum_fusion.5), channel_id=1, source_target_pairs={{0,24},{8,0},{16,8},{24,16},{32,56},{40,32},{48,40},{56,48},{64,88... | collective-permute-start | bytes 1204232 | tf_op jit(solution)/shard_map/ppermute | solution.py:44
  83.6 4.6 %copy-start.2 = (bf16[1040,128]{1,0:T(8,128)(2,1)}, bf16[1040,128]{1,0:T(8,128)(2,1)S(1)}, u32[]{:S(2)}) copy-start(bf16[1040,128]{1,0:T(8,128)(2,1)S(1)} %collective-permute-done.9.refs_2_) | copy-start | bytes 798724
  83.6 17.1 %collective-permute-start.10 = (bf16[1040,128]{1,0:T(8,128)(2,1)S(1)}, bf16[1040,128]{1,0:T(8,128)(2,1)S(1)}, u32[]{:S(2)}, u32[]{:S(2)}) collective-permute-start(bf16[1040,128]{1,0:T(8,128)(2,1)S(1)} %collective-permute-done.9.refs_2_), channel_id=1, source_target_pairs={{0,32},{8,40},{16,48},{24,56},{32,64},{40,72},{48,80},{56,88},{64,... | collective-permute-start | bytes 798728 | tf_op jit(solution)/shard_map/ppermute | solution.py:38
  83.7 4.5 %copy-start.16 = (bf16[1552,128]{1,0:T(8,128)(2,1)}, bf16[1552,128]{1,0:T(8,128)(2,1)S(1)}, u32[]{:S(2)}) copy-start(bf16[1552,128]{1,0:T(8,128)(2,1)S(1)} %collective-permute-done.13.refs_0_) | copy-start | bytes 1191940
  83.8 16.9 %collective-permute-start.14 = (bf16[1552,128]{1,0:T(8,128)(2,1)S(1)}, bf16[1552,128]{1,0:T(8,128)(2,1)S(1)}, u32[]{:S(2)}, u32[]{:S(2)}) collective-permute-start(bf16[1552,128]{1,0:T(8,128)(2,1)S(1)} %pad_maximum_fusion.10), channel_id=1, source_target_pairs={{0,8},{8,16},{16,24},{24,0},{32,40},{40,48},{48,56},{56,32},{64,72... | collective-permute-start | bytes 1191944 | tf_op jit(solution)/shard_map/ppermute | solution.py:44
  83.9 4.4 %copy-start.12 = (bf16[1568,128]{1,0:T(8,128)(2,1)}, bf16[1568,128]{1,0:T(8,128)(2,1)S(1)}, u32[]{:S(2)}) copy-start(bf16[1568,128]{1,0:T(8,128)(2,1)S(1)} %collective-permute-done.19.refs_1_) | copy-start | bytes 1204228
  83.9 17.5 %collective-permute-start.20 = (bf16[1568,128]{1,0:T(8,128)(2,1)S(1)}, bf16[1568,128]{1,0:T(8,128)(2,1)S(1)}, u32[]{:S(2)}, u32[]{:S(2)}) collective-permute-start(bf16[1568,128]{1,0:T(8,128)(2,1)S(1)} %pad_maximum_fusion.6), channel_id=1, source_target_pairs={{0,24},{8,0},{16,8},{24,16},{32,56},{40,32},{48,40},{56,48},{64,88... | collective-permute-start | bytes 1204232 | tf_op jit(solution)/shard_map/ppermute | solution.py:44
  100.7 3.8 %copy-start.17 = (bf16[1552,128]{1,0:T(8,128)(2,1)}, bf16[1552,128]{1,0:T(8,128)(2,1)S(1)}, u32[]{:S(2)}) copy-start(bf16[1552,128]{1,0:T(8,128)(2,1)S(1)} %collective-permute-done.14.refs_0_) | copy-start | bytes 1191940
  100.7 3.7 %copy-start.3 = (bf16[1040,128]{1,0:T(8,128)(2,1)}, bf16[1040,128]{1,0:T(8,128)(2,1)S(1)}, u32[]{:S(2)}) copy-start(bf16[1040,128]{1,0:T(8,128)(2,1)S(1)} %collective-permute-done.10.refs_2_) | copy-start | bytes 798724
  100.8 14.0 %collective-permute-start.15 = (bf16[1552,128]{1,0:T(8,128)(2,1)S(1)}, bf16[1552,128]{1,0:T(8,128)(2,1)S(1)}, u32[]{:S(2)}, u32[]{:S(2)}) collective-permute-start(bf16[1552,128]{1,0:T(8,128)(2,1)S(1)} %pad_maximum_fusion.11), channel_id=1, source_target_pairs={{0,8},{8,16},{16,24},{24,0},{32,40},{40,48},{48,56},{56,32},{64,72... | collective-permute-start | bytes 1191944 | tf_op jit(solution)/shard_map/ppermute | solution.py:44
  101.4 3.0 %copy-start.13 = (bf16[1568,128]{1,0:T(8,128)(2,1)}, bf16[1568,128]{1,0:T(8,128)(2,1)S(1)}, u32[]{:S(2)}) copy-start(bf16[1568,128]{1,0:T(8,128)(2,1)S(1)} %collective-permute-done.20.refs_1_) | copy-start | bytes 1204228
  101.5 13.4 %collective-permute-start.21 = (bf16[1568,128]{1,0:T(8,128)(2,1)S(1)}, bf16[1568,128]{1,0:T(8,128)(2,1)S(1)}, u32[]{:S(2)}, u32[]{:S(2)}) collective-permute-start(bf16[1568,128]{1,0:T(8,128)(2,1)S(1)} %pad_maximum_fusion.7), channel_id=1, source_target_pairs={{0,24},{8,0},{16,8},{24,16},{32,56},{40,32},{48,40},{56,48},{64,88... | collective-permute-start | bytes 1204232 | tf_op jit(solution)/shard_map/ppermute | solution.py:44
  114.8 3.4 %copy-start.18 = (bf16[1552,128]{1,0:T(8,128)(2,1)}, bf16[1552,128]{1,0:T(8,128)(2,1)S(1)}, u32[]{:S(2)}) copy-start(bf16[1552,128]{1,0:T(8,128)(2,1)S(1)} %collective-permute-done.15.refs_0_) | copy-start | bytes 1191940
  114.8 11.6 %collective-permute-start.16 = (bf16[512,128]{1,0:T(8,128)(2,1)S(1)}, bf16[512,128]{1,0:T(8,128)(2,1)S(1)}, u32[]{:S(2)}, u32[]{:S(2)}) collective-permute-start(bf16[512,128]{1,0:T(8,128)(2,1)S(1)} %slice.121), channel_id=1, source_target_pairs={{0,8},{8,16},{16,24},{24,0},{32,40},{40,48},{48,56},{56,32},{64,72... | collective-permute-start | bytes 393224 | tf_op jit(solution)/shard_map/ppermute | solution.py:44
  114.9 3.3 %copy-start.14 = (bf16[1568,128]{1,0:T(8,128)(2,1)}, bf16[1568,128]{1,0:T(8,128)(2,1)S(1)}, u32[]{:S(2)}) copy-start(bf16[1568,128]{1,0:T(8,128)(2,1)S(1)} %collective-permute-done.21.refs_1_) | copy-start | bytes 1204228
  115.0 11.4 %collective-permute-start.22 = (bf16[528,128]{1,0:T(8,128)(2,1)S(1)}, bf16[528,128]{1,0:T(8,128)(2,1)S(1)}, u32[]{:S(2)}, u32[]{:S(2)}) collective-permute-start(bf16[528,128]{1,0:T(8,128)(2,1)S(1)} %slice.126), channel_id=1, source_target_pairs={{0,24},{8,0},{16,8},{24,16},{32,56},{40,32},{48,40},{56,48},{64,88... | collective-permute-start | bytes 405512 | tf_op jit(solution)/shard_map/ppermute | solution.py:44
  126.4 0.6 copy-start.21
  126.4 0.7 copy-start.20
  135.5 17.9 %collective-permute-start.23 = (bf16[3,512,512]{2,1,0:T(8,128)(2,1)}, bf16[3,512,512]{2,1,0:T(8,128)(2,1)S(1)}, u32[]{:S(2)}, u32[]{:S(2)}) collective-permute-start(bf16[3,512,512]{2,1,0:T(8,128)(2,1)} %get-tuple-element.76), channel_id=1, source_target_pairs={{0,1},{1,0},{2,3},{3,2},{4,5},{5,4},{6,7},{7,6},{8,9},{9,8},{10,11... | collective-permute-start | bytes 4718600 | tf_op jit(solution)/shard_map/ppermute | solution.py:34
  135.6 4.4 %collective-permute-start.24 = (bf16[512,512]{1,0:T(8,128)(2,1)}, bf16[512,512]{1,0:T(8,128)(2,1)S(1)}, u32[]{:S(2)}, u32[]{:S(2)}) collective-permute-start(bf16[512,512]{1,0:T(8,128)(2,1)} %get-tuple-element.78), channel_id=1, source_target_pairs={{0,1},{1,0},{2,3},{3,2},{4,5},{5,4},{6,7},{7,6},{8,9},{9,8},{10,11... | collective-permute-start | bytes 1572872 | tf_op jit(solution)/shard_map/ppermute | solution.py:34
  141.4 8.6 %collective-permute-start.25 = (bf16[256,512]{1,0:T(8,128)(2,1)S(1)}, bf16[256,512]{1,0:T(8,128)(2,1)S(1)}, u32[]{:S(2)}, u32[]{:S(2)}) collective-permute-start(bf16[256,512]{1,0:T(8,128)(2,1)S(1)} %get-tuple-element.89), channel_id=1, source_target_pairs={{0,2},{2,4},{4,6},{6,0},{1,3},{3,5},{5,7},{7,1},{8,10},{10,12},{12... | collective-permute-start | bytes 786440 | tf_op jit(solution)/shard_map/ppermute | solution.py:34
  144.1 9.3 %collective-permute-start.29 = (bf16[256,512]{1,0:T(8,128)(2,1)S(1)}, bf16[256,512]{1,0:T(8,128)(2,1)S(1)}, u32[]{:S(2)}, u32[]{:S(2)}) collective-permute-start(bf16[256,512]{1,0:T(8,128)(2,1)S(1)} %get-tuple-element.90), channel_id=1, source_target_pairs={{0,6},{2,0},{4,2},{6,4},{1,7},{3,1},{5,3},{7,5},{8,14},{10,8},{12,... | collective-permute-start | bytes 786440 | tf_op jit(solution)/shard_map/ppermute | solution.py:34
  154.8 9.3 %collective-permute-start.26 = (bf16[256,512]{1,0:T(8,128)(2,1)S(1)}, bf16[256,512]{1,0:T(8,128)(2,1)S(1)}, u32[]{:S(2)}, u32[]{:S(2)}) collective-permute-start(bf16[256,512]{1,0:T(8,128)(2,1)S(1)} %get-tuple-element.83), channel_id=1, source_target_pairs={{0,2},{2,4},{4,6},{6,0},{1,3},{3,5},{5,7},{7,1},{8,10},{10,12},{12... | collective-permute-start | bytes 786440 | tf_op jit(solution)/shard_map/ppermute | solution.py:34
  155.1 10.4 %collective-permute-start.30 = (bf16[256,512]{1,0:T(8,128)(2,1)S(1)}, bf16[256,512]{1,0:T(8,128)(2,1)S(1)}, u32[]{:S(2)}, u32[]{:S(2)}) collective-permute-start(bf16[256,512]{1,0:T(8,128)(2,1)S(1)} %get-tuple-element.84), channel_id=1, source_target_pairs={{0,6},{2,0},{4,2},{6,4},{1,7},{3,1},{5,3},{7,5},{8,14},{10,8},{12,... | collective-permute-start | bytes 786440 | tf_op jit(solution)/shard_map/ppermute | solution.py:34
  158.3 10.9 %collective-permute-start.27 = (bf16[256,512]{1,0:T(8,128)(2,1)S(1)}, bf16[256,512]{1,0:T(8,128)(2,1)S(1)}, u32[]{:S(2)}, u32[]{:S(2)}) collective-permute-start(bf16[256,512]{1,0:T(8,128)(2,1)S(1)} %get-tuple-element.85), channel_id=1, source_target_pairs={{0,6},{2,0},{4,2},{6,4},{1,7},{3,1},{5,3},{7,5},{8,14},{10,8},{12,... | collective-permute-start | bytes 786440 | tf_op jit(solution)/shard_map/ppermute | solution.py:34
  158.3 10.8 %collective-permute-start.28 = (bf16[256,512]{1,0:T(8,128)(2,1)S(1)}, bf16[256,512]{1,0:T(8,128)(2,1)S(1)}, u32[]{:S(2)}, u32[]{:S(2)}) collective-permute-start(bf16[256,512]{1,0:T(8,128)(2,1)S(1)} %get-tuple-element.86), channel_id=1, source_target_pairs={{0,2},{2,4},{4,6},{6,0},{1,3},{3,5},{5,7},{7,1},{8,10},{10,12},{12... | collective-permute-start | bytes 786440 | tf_op jit(solution)/shard_map/ppermute | solution.py:34
where the time goes:
time: 171 us; the launch traced here: 170 us
  Pallas kernels  77.4 us (45%)
  starting transfers between devices  38.4 us (22%)
  waiting for transfers between devices  31.5 us (18%)
  other arithmetic  13.5 us (8%)
  local copies, waits for them, and re-layouts  8.92 us (5%)
    pallas_call x5, Pallas kernels, attend_stage(): pl.pallas_call(kernel, out_shape=STATE, in_specs=[smem()] + vmem(1) + [pl...  47 us
    ppermute x15, waiting for transfers between devices, shift(): return lax.ppermute(x, axis, [(i, (i + distance) % n) for i in range(n)])  27.6 us
    ppermute x12, starting transfers between devices, shift_y(): lax.ppermute(x, 'tok', [(z * Y + y, z * Y + (y + distance) % Y) for z in...  23 us
    ppermute x15, starting transfers between devices, shift(): return lax.ppermute(x, axis, [(i, (i + distance) % n) for i in range(n)])  14.3 us
    pallas_call x1, Pallas kernels, project(): pl.pallas_call(project_kernel, out_shape=(jax.ShapeDtypeStruct((GROUP * H...  12 us
    pallas_call x1, Pallas kernels, finish(): pl.pallas_call(kernel, out_shape=(jax.ShapeDtypeStruct((T, GROUP * HEAD_S...  8.35 us
    pallas_call x1, Pallas kernels, own_products(): pl.pallas_call(kernel, out_shape=jax.ShapeDtypeStruct((3, T, PIECE), f32)...  5.06 us
    pallas_call x1, Pallas kernels, attend_first(): pl.pallas_call(kernel, out_shape=STATE, in_specs=vmem(4), out_specs=tuple...  4.98 us
  transfers between devices with their start and end apart: 31, of which 14 were waited for; matrix products, arithmetic and copies ran while one was open for 10% of the time, Pallas kernels for 34%

commit v1 on v0

--- a/solution.py
+++ b/solution.py
@@ -97,7 +97,7 @@
                 normed[pl.ds(half * HALF + row, step_rows), pl.ds(column, PIECE)] = v.astype(bf16)
             return 0
 
-        lax.fori_loop(0, HALF // step_rows, step, 0)
+        lax.fori_loop(0, HALF // step_rows, step, 0, unroll=4)
 
     def columns(i, _):
         for j in range(3):
@@ -202,12 +202,11 @@
     return copies
 
 
-def attend_earlier(info, which, sources, queries, blocks, bias, sems, fill, state):
+def attend_earlier(info, indices, sources, queries, blocks, bias, sems, fill, state):
     own, first_doc = info[0], info[1].astype(f32)
 
     def reached(j):
-        index = info[3 + which[j]]
-        return (index >= 0) & (index < own)
+        return (indices[j] >= 0) & (indices[j] < own)
 
     def each(j, act):
         def run():
@@ -216,18 +215,18 @@
 
         return run
 
-    for j in range(len(which)):
+    for j in range(len(indices)):
         pl.when(reached(j))(each(j, lambda copy: copy.start()))
     fill()
 
     def step(k, _):
         wanted = reached(0)
-        for j in range(1, len(which)):
+        for j in range(1, len(indices)):
             wanted = jnp.where(k == j, reached(j), wanted)
 
         @pl.when(wanted)
         def _():
-            for j in range(len(which)):
+            for j in range(len(indices)):
                 pl.when(k == j)(each(j, lambda copy: copy.wait()))
             block = blocks.at[k]
             ids = block[KV_ROWS:MSG_ROWS, :].astype(f32)
@@ -237,14 +236,14 @@
             def _():
                 key = lax.broadcasted_iota(jnp.int32, (T, LANES), 0)
                 bias[...] = jnp.where(key < low, floor_score, 0.0)
-                attend_block(block, queries, *state, lambda scores, at: scores + bias[...], 1 if len(which) == 3 and which[0] == 3 else TOGETHER)
+                attend_block(block, queries, *state, lambda scores, at: scores + bias[...], TOGETHER)
 
         return 0
 
-    lax.fori_loop(0, len(which), step, 0)
-
-
-TOGETHER = 2
+    lax.fori_loop(0, len(indices), step, 0)
+
+
+TOGETHER = 4
 STATE = (
     jax.ShapeDtypeStruct((GROUP, 1, T), f32),
     jax.ShapeDtypeStruct((GROUP, 1, T), f32),
@@ -286,43 +285,46 @@
     )(message, queries, doc_rows, doc_columns)
 
 
-def attend_stage(info, queries, state, along, against, straight, between, which):
+def attend_stage(number, info, queries, state, along, against, straight):
     n = 2 + (straight is not None)
 
-    def kernel(info, queries, *refs):
-        refs = list(refs)
-        messages = [refs.pop(0) for _ in range(n)]
-        old = [refs.pop(0) for _ in state]
-        new = [refs.pop(0) for _ in range(3)]
+    def kernel(number, info, queries, *refs):
+        messages, old, new, refs = refs[:n], refs[n : n + 3], refs[n + 3 : n + 6], refs[n + 6 :]
 
         def fill():
-            if old:
-                for a, b in zip(old, new):
-                    b[...] = a[...]
-            else:
-                clear(*new)
-
-        sources = [whole_of(m) for m in messages]
-        if between:
-            sources.append(pair_of(messages[0], MSG_ROWS, messages[1], MSG_ROWS))
-        attend_earlier(info, which, sources, queries, *refs, fill, new)
+            for a, b in zip(old, new):
+                b[...] = a[...]
+
+        s = number[0]
+        two_away = info[jnp.maximum(3 + 4 * s - 2, 3)]
+        indices = [info[3 + 4 * s + 3], info[3 + 4 * s + 1]]
+        indices.append(jnp.where(s > 0, two_away, -1))
+        sources = [whole_of(messages[0]), whole_of(messages[1])]
+        sources.append(pair_of(messages[0], MSG_ROWS, messages[1], MSG_ROWS))
+        if straight is not None:
+            indices.append(info[3 + 4 * s + 4])
+            sources.append(whole_of(messages[2]))
+        attend_earlier(info, indices, sources, queries, *refs, fill, new)
 
     messages = [along, against] + ([straight] if straight is not None else [])
     return pl.pallas_call(
         kernel,
         out_shape=STATE,
-        in_specs=[smem()] + vmem(1) + [pl.BlockSpec(memory_space=pl.ANY)] * n + vmem(len(state)),
+        in_specs=[smem(), smem()]
+        + vmem(1)
+        + [pl.BlockSpec(memory_space=pl.ANY)] * n
+        + vmem(3),
         out_specs=tuple(vmem(3)),
-        scratch_shapes=earlier_scratch(len(which)),
-        input_output_aliases={2 + n + i: i for i in range(len(state))},
+        scratch_shapes=earlier_scratch(1 + n),
+        input_output_aliases={3 + n + i: i for i in range(3)},
         compiler_params=params(),
         cost_estimate=pl.CostEstimate(
-            flops=2 * len(which) * BLOCK_FLOPS,
-            transcendentals=len(which) * GROUP * T * T,
+            flops=2 * (1 + n) * BLOCK_FLOPS,
+            transcendentals=(1 + n) * GROUP * T * T,
             bytes_accessed=3 << 20,
         ),
         name="attend_stage",
-    )(info, queries, *messages, *state)
+    )(number, info, queries, *messages, *state)
 
 
 def fetch_columns(columns, first, count, weight, held, sems):
@@ -342,13 +344,13 @@
     ]
 
 
-def finish(info, queries, own_state, state, keys, values, which, columns, weight):
+def finish(info, queries, own_state, state, keys, values, columns, weight):
     def kernel(
         info, columns, queries, keys, values, own_highest, own_totals, own_accum,
         old_highest, old_totals, old_accum, weight,
-        heads, first, others, far, highest, totals, accum, blocks, bias, sems, held, held_sems,
+        heads, first, far, highest, totals, accum, blocks, bias, sems, held, held_sems,
     ):
-        fetches = fetch_columns(columns, 0, 5, weight, held, held_sems)
+        fetches = fetch_columns(columns, 0, 2, weight, held, held_sems)
 
         def fill():
             highest[...] = old_highest[...]
@@ -356,7 +358,7 @@
             accum[...] = old_accum[...]
 
         attend_earlier(
-            info, which, [pair_of(keys, 0, values, 0)], queries, blocks, bias, sems, fill,
+            info, [info[3 + 4 * 4 + 2]], [pair_of(keys, 0, values, 0)], queries, blocks, bias, sems, fill,
             (highest, totals, accum),
         )
         query = lax.broadcasted_iota(jnp.int32, (1, T), 1)
@@ -370,30 +372,16 @@
             total = own_totals[h] * near + totals[h] * past
             summed = own_accum[rows, :] * near + accum[rows, :] * past
             heads[:, rows] = (summed / total).astype(bf16).T
-
-        def multiply(k, _):
-            for j in range(5):
-                pl.when(k == j)(fetches[j].wait)
-            far[...] = jnp.dot(heads[...], held[k], preferred_element_type=f32)
-
-            @pl.when(k == 0)
-            def _():
-                first[...] = far[...].astype(bf16)
-
-            @pl.when((k > 0) & (k < 4))
-            def _():
-                others[jnp.clip(k - 1, 0, 2)] = far[...].astype(bf16)
-
-            return 0
-
-        lax.fori_loop(0, 5, multiply, 0)
+        for fetch in fetches:
+            fetch.wait()
+        first[...] = jnp.dot(heads[...], held[0], preferred_element_type=f32).astype(bf16)
+        far[...] = jnp.dot(heads[...], held[1], preferred_element_type=f32)
 
     return pl.pallas_call(
         kernel,
         out_shape=(
             jax.ShapeDtypeStruct((T, GROUP * HEAD_SIZE), bf16),
             jax.ShapeDtypeStruct((T, PIECE), bf16),
-            jax.ShapeDtypeStruct((3, T, PIECE), bf16),
             jax.ShapeDtypeStruct((T, PIECE), f32),
         ),
         in_specs=[smem(), smem()]
@@ -401,14 +389,14 @@
         + [pl.BlockSpec(memory_space=pl.ANY)] * 2
         + vmem(6)
         + [pl.BlockSpec(memory_space=pl.ANY)],
-        out_specs=tuple(vmem(4)),
+        out_specs=tuple(vmem(3)),
         scratch_shapes=[
             pltpu.VMEM((GROUP, 1, T), f32),
             pltpu.VMEM((GROUP, 1, T), f32),
             pltpu.VMEM((GROUP * HEAD_SIZE, T), f32),
         ]
         + earlier_scratch(1)
-        + column_scratch(5),
+        + column_scratch(2),
         compiler_params=params(),
         cost_estimate=pl.CostEstimate(
             flops=2 * T * T * MODEL_WIDTH, transcendentals=0, bytes_accessed=8 << 20
@@ -417,21 +405,21 @@
     )(info, columns, queries, keys, values, *own_state, *state, weight)
 
 
-def own_products(columns, heads, weight):
+def three_products(columns, start, heads, weight, dtype):
     def kernel(columns, heads, weight, out, held, sems):
-        fetches = fetch_columns(columns, 5, 3, weight, held, sems)
+        fetches = fetch_columns(columns, start, 3, weight, held, sems)
 
         def multiply(k, _):
             for j in range(3):
                 pl.when(k == j)(fetches[j].wait)
-            out[k] = jnp.dot(heads[...], held[k], preferred_element_type=f32)
+            out[k] = jnp.dot(heads[...], held[k], preferred_element_type=f32).astype(dtype)
             return 0
 
         lax.fori_loop(0, 3, multiply, 0)
 
     return pl.pallas_call(
         kernel,
-        out_shape=jax.ShapeDtypeStruct((3, T, PIECE), f32),
+        out_shape=jax.ShapeDtypeStruct((3, T, PIECE), dtype),
         in_specs=[smem()] + vmem(1) + [pl.BlockSpec(memory_space=pl.ANY)],
         out_specs=vmem(1)[0],
         scratch_shapes=column_scratch(3),
@@ -439,7 +427,7 @@
         cost_estimate=pl.CostEstimate(
             flops=2 * T * T * MODEL_WIDTH // 2, transcendentals=0, bytes_accessed=6 << 20
         ),
-        name="own_products",
+        name="three_products",
     )(columns, heads, weight)
 
 
@@ -474,57 +462,65 @@
         [shard, doc_ids[0], jnp.sum((doc_ids == doc_ids[0]).astype(jnp.int32))] + blocks
     ).astype(jnp.int32)
     order = jnp.stack([(chip + 2) % 4, (chip + 1) % 4, (chip + 3) % 4, chip])
-    columns = jnp.concatenate([order * 2 + 1 - core, order * 2 + core]).astype(jnp.int32)
-
-    behind, ahead, across = lax.optimization_barrier((behind, ahead, across))
+    columns = jnp.concatenate(
+        [order[:1] * 2 + 1 - core, order[:1] * 2 + core, order[1:] * 2 + 1 - core, order[1:] * 2 + core]
+    ).astype(jnp.int32)
+
+    behind, ahead, across, fids, info, columns, cosine, sine, ids = lax.optimization_barrier(
+        (behind, ahead, across, fids, info, columns, cosine, sine, ids)
+    )
     top = shift(behind[:HALF], "head", 1)
     bottom = shift(ahead[HALF:], "head", -1)
     across_near = shift(jnp.concatenate([behind, ahead]), "grp", 1)
-    top, bottom, fids, info, columns, cosine, sine, ids, doc_rows, doc_columns = (
-        lax.optimization_barrier(
-            (top, bottom, fids, info, columns, cosine, sine, ids, doc_rows, doc_columns)
-        )
+    top, bottom, doc_rows, doc_columns = lax.optimization_barrier(
+        (top, bottom, doc_rows, doc_columns)
     )
     mine = [own, behind, ahead, top, bottom]
     across_far = shift(jnp.concatenate([top, bottom]), "grp", 1)
     theirs = [across, across_near, across_far]
     queries, message = project(fids, mine + theirs, query_key_value_weight, cosine, sine, ids)
 
-    straight = message
+    state = (
+        jnp.full((GROUP, 1, T), floor_score, f32),
+        jnp.zeros((GROUP, 1, T), f32),
+        jnp.zeros((GROUP * HEAD_SIZE, T), f32),
+    )
+    along, against = shift_y(message, 1), shift_y(message, -1)
+    straight = shift_z(message)
     own_state = attend_first(queries, message, doc_rows, doc_columns)
-    state = ()
-    along, against = message, message
-    for s in range(5):
-        next_along = shift_y(along, 1)
-        next_against = shift_y(against, -1)
-        following = shift_z(straight) if s < 4 else None
-        which = [4 * s + 3, 4 * s + 1]
-        if s < 4:
-            which.append(4 * (s + 1))
-        if s > 0:
-            which.append(4 * (s - 1) + 2)
-        state = attend_stage(
-            info, queries, state, next_along, next_against, following, s > 0, which
-        )
-        forward, backward = next_along[0:T], next_against[T:MSG_ROWS]
-        if s < 4:
-            straight = following
-            along = jnp.concatenate([straight, forward], axis=0)
-            against = jnp.concatenate([straight, backward], axis=0)
-    keys = shift_y(forward, 1)
-    values = shift_y(backward, -1)
-
-    heads, first, others, products = finish(
-        info, queries, own_state, state, keys, values, [4 * 4 + 2], columns, out_weight
+    along = jnp.pad(along, ((0, T), (0, 0)))
+    against = jnp.pad(against, ((0, MSG_ROWS - T), (0, 0)))
+
+    def stage(s, carried):
+        along, against, straight, state = carried
+        next_along = shift_y(jnp.concatenate([straight, along[:T]]), 1)
+        next_against = shift_y(jnp.concatenate([straight, against[T:MSG_ROWS]]), -1)
+        following = shift_z(straight)
+        number = jnp.full((1,), s - 1, jnp.int32)
+        state = attend_stage(number, info, queries, state, along, against, straight)
+        return next_along, next_against, following, state
+
+    along, against, straight, state = lax.fori_loop(
+        1, 5, stage, (along, against, straight, state)
+    )
+    keys = shift_y(along[:T], 1)
+    values = shift_y(against[T:MSG_ROWS], -1)
+    state = attend_stage(
+        jnp.full((1,), 4, jnp.int32), info, queries, state, along, against, None
+    )
+
+    heads, first, products = finish(
+        info, queries, own_state, state, keys, values, columns, out_weight
     )
     first = shift(first, "grp", 1)
+    others = three_products(columns, 2, heads, out_weight, bf16)
     others = shift(others, "grp", 1)
-    own_three = own_products(columns, heads, out_weight)
 
     far = (products + first.astype(f32)).astype(bf16)
     far_up = shift(far[:HALF], "head", 1)
     far_down = shift(far[HALF:], "head", -1)
-    products = own_three
+    heads, far = lax.optimization_barrier((heads, far))
+    products = three_products(columns, 5, heads, out_weight, f32)
     up_low = (products[0, HALF:] + others[0, HALF:].astype(f32)).astype(bf16)
     down_high = (products[1, :HALF] + others[1, :HALF].astype(f32)).astype(bf16)
     up_low = shift(up_low, "head", 1)

time: 171 us -> 168 us (0.982)
  the two profiles are of different devices: /device:TPU:134 before, /device:TPU:8 now
where the time goes in v1:
time: 168 us; the launch traced here: 165 us
  waiting for transfers between devices  58.8 us (35%)
  Pallas kernels  42.8 us (25%)
  starting transfers between devices  41.5 us (25%)
  other arithmetic  11.6 us (7%)
  local copies, waits for them, and re-layouts  9.5 us (6%)
    ppermute x12, waiting for transfers between devices, shift_y(): lax.ppermute(x, 'tok', [(z * Y + y, z * Y + (y + distance) % Y) for z in...  27.8 us
    ppermute x15, waiting for transfers between devices, shift(): return lax.ppermute(x, axis, [(i, (i + distance) % n) for i in range(n)])  26.9 us
    ppermute x15, starting transfers between devices, shift(): return lax.ppermute(x, axis, [(i, (i + distance) % n) for i in range(n)])  16.1 us
    ppermute x12, starting transfers between devices, shift_y(): lax.ppermute(x, 'tok', [(z * Y + y, z * Y + (y + distance) % Y) for z in...  16 us
    pallas_call x5, Pallas kernels, attend_stage(): pl.pallas_call(kernel, out_shape=STATE, in_specs=[smem(), smem()] + vmem(...  14.1 us
    pallas_call x2, Pallas kernels, three_products(): pl.pallas_call(kernel, out_shape=jax.ShapeDtypeStruct((3, T, PIECE), dtyp...  9.79 us
    pallas_call x1, Pallas kernels, project(): pl.pallas_call(project_kernel, out_shape=(jax.ShapeDtypeStruct((GROUP * H...  9.62 us
    ppermute x5, starting transfers between devices, shift_z(): lax.ppermute(x, 'tok', [(z * Y + y, (z + 1) % Z * Y + y) for z in range(Z...  9.38 us
  transfers between devices with their start and end apart: 32, of which 16 were waited for; matrix products, arithmetic and copies ran while one was open for 8% of the time, Pallas kernels for 15%

profile of v1, /device:TPU:8, one launch (start us, length us, event | category | flops | bytes accessed | tf_op | source)
XLA Modules:
  0.0 164.9 jit_solution(18091568399450650887)
XLA Ops:
  0.0 0.7 broadcast_in_dim.14
  0.7 1.1 pad_maximum_fusion.3.x0
  1.8 1.6 collective-permute-start.3
  3.3 1.7 %collective-permute-start.4 = (bf16[528,512]{1,0:T(8,128)(2,1)S(1)}, bf16[528,512]{1,0:T(8,128)(2,1)S(1)}, u32[]{:S(2)}, u32[]{:S(2)}) collective-permute-start(bf16[528,512]{1,0:T(8,128)(2,1)S(1)} %pad_maximum_fusion.3.x0), channel_id=1, source_target_pairs={{0,6},{2,0},{4,2},{6,4},{1,7},{3,1},{5,3},{7,5},{8,14},{10,8},{12,... | collective-permute-start | bytes 1622024 | tf_op jit(solution)/shard_map/ppermute | solution.py:34
  5.1 1.3 slice.93
  6.3 2.0 %fusion.18 = (f32[512]{0:T(512)S(1)}, s32[]{:T(128)}, bf16[4,128]{1,0:T(4,128)(2,1)S(1)}) fusion(s32[512]{0:T(512)} %param.11, s32[]{:T(128)} %bitcast.6), kind=kLoop, calls=%fused_computation.48 | loop fusion | flops 2559 | bytes 5128 | tf_op jit(solution)/shard_map/convert_element_type | solution.py:457
  8.5 0.6 concatenate.60.ids
  9.1 0.6 pad_add_fusion
  9.7 1.3 stack.120.info
  11.1 1.0 fusion.16
  12.1 1.0 pad_maximum_fusion.6
  13.1 4.0 %collective-permute-done.3.p0 = bf16[528,512]{1,0:T(8,128)(2,1)S(1)} collective-permute-done((bf16[528,512]{1,0:T(8,128)(2,1)S(1)}, bf16[528,512]{1,0:T(8,128)(2,1)S(1)}, u32[]{:S(2)}, u32[]{:S(2)}) %collective-permute-start.3) | collective-permute-done | bytes 540704 | tf_op jit(solution)/shard_map/ppermute | solution.py:34
  17.3 3.0 %collective-permute-start.7 = (bf16[272,512]{1,0:T(8,128)(2,1)S(1)}, bf16[272,512]{1,0:T(8,128)(2,1)S(1)}, u32[]{:S(2)}, u32[]{:S(2)}) collective-permute-start(bf16[272,512]{1,0:T(8,128)(2,1)S(1)} %slice.95), channel_id=1, source_target_pairs={{0,6},{2,0},{4,2},{6,4},{1,7},{3,1},{5,3},{7,5},{8,14},{10,8},{12,... | collective-permute-start | bytes 835592 | tf_op jit(solution)/shard_map/ppermute | solution.py:34
  20.5 9.6 %collective-permute-done.6.q0 = bf16[256,512]{1,0:T(8,128)(2,1)S(1)} collective-permute-done((bf16[256,512]{1,0:T(8,128)(2,1)S(1)}, bf16[256,512]{1,0:T(8,128)(2,1)S(1)}, u32[]{:S(2)}, u32[]{:S(2)}) %collective-permute-start.6) | collective-permute-done | bytes 262176 | tf_op jit(solution)/shard_map/ppermute | solution.py:34
  30.1 0.9 broadcast_in_dim.15.doc_rows
  31.0 0.6 broadcast_in_dim.16.doc_columns
  31.7 1.9 %collective-permute-done.9.qr1 = bf16[528,512]{1,0:T(8,128)(2,1)S(1)} collective-permute-done((bf16[528,512]{1,0:T(8,128)(2,1)S(1)}, bf16[528,512]{1,0:T(8,128)(2,1)S(1)}, u32[]{:S(2)}, u32[]{:S(2)}) %collective-permute-start.9) | collective-permute-done | bytes 540704 | tf_op jit(solution)/shard_map/ppermute | solution.py:34
  33.7 0.8 copy-done.9
  34.4 1.0 copy-done.7
  35.4 9.6 %project.1 = (bf16[512,512]{1,0:T(8,128)(2,1)S(1)}, bf16[1040,128]{1,0:T(8,128)(2,1)}) custom-call(s32[8]{0:T(128)} %get-tuple-element.327.fids, bf16[528,512]{1,0:T(8,128)(2,1)} %copy-done.4, bf16[528,512]{1,0:T(8,128)(2,1)} %copy-done.2, bf16[528,512]{1,0:T(8,128)(2,1)} %copy-done.1, bf16[256,512]{1,0:T(8,128)(2,1)} %copy-done.6, ...), custom_call_target="tpu_custom_call" | custom-call | flops 3221225472 | bytes 12582912 | tf_op jit(solution)/shard_map/project/pallas_call | solution.py:126
  45.1 0.4 collective-permute-start.11
  45.5 1.7 %collective-permute-start.10 = (bf16[1040,128]{1,0:T(8,128)(2,1)}, bf16[1040,128]{1,0:T(8,128)(2,1)S(1)}, u32[]{:S(2)}, u32[]{:S(2)}) collective-permute-start(bf16[1040,128]{1,0:T(8,128)(2,1)} %get-tuple-element.337.message), channel_id=1, source_target_pairs={{0,8},{8,16},{16,24},{24,0},{32,40},{40,48},{48,56},{56,32},{64,72... | collective-permute-start | bytes 798728 | tf_op jit(solution)/shard_map/ppermute | solution.py:44
  47.2 1.9 %collective-permute-start.12 = (bf16[1040,128]{1,0:T(8,128)(2,1)}, bf16[1040,128]{1,0:T(8,128)(2,1)S(1)}, u32[]{:S(2)}, u32[]{:S(2)}) collective-permute-start(bf16[1040,128]{1,0:T(8,128)(2,1)} %get-tuple-element.337.message), channel_id=1, source_target_pairs={{0,32},{8,40},{16,48},{24,56},{32,64},{40,72},{48,80},{56,88},{64,... | collective-permute-start | bytes 798728 | tf_op jit(solution)/shard_map/ppermute | solution.py:38
  49.1 4.8 %attend_own.1 = (f32[4,1,512]{2,1,0:T(1,128)}, f32[4,1,512]{2,1,0:T(1,128)}, f32[512,512]{1,0:T(8,128)}) custom-call(bf16[1040,128]{1,0:T(8,128)(2,1)} %get-tuple-element.337.message, bf16[512,512]{1,0:T(8,128)(2,1)S(1)} %get-tuple-element.464.queries, f32[512,128]{1,0:T(8,128)} %broadcast_in_dim.15.doc_rows, f32[8,512]{1,0:T(8,128)} %broadcast_in_dim.16.doc_columns), custom_call_target="tpu_custom_call" | custom-call | flops 1073741824 | bytes 2097152 | tf_op jit(solution)/shard_map/attend_own/pallas_call | solution.py:275
  53.9 1.4 collective-permute-done.10
  55.3 4.1 %collective-permute-done.12 = bf16[1040,128]{1,0:T(8,128)(2,1)S(1)} collective-permute-done((bf16[1040,128]{1,0:T(8,128)(2,1)}, bf16[1040,128]{1,0:T(8,128)(2,1)S(1)}, u32[]{:S(2)}, u32[]{:S(2)}) %collective-permute-start.12) | collective-permute-done | bytes 266272 | tf_op jit(solution)/shard_map/ppermute | solution.py:38
  59.4 1.1 broadcast_in_dim.38
  60.5 56.7 %while.27 = (s32[]{:T(128)}, bf16[1552,128]{1,0:T(8,128)(2,1)S(1)}, bf16[1568,128]{1,0:T(8,128)(2,1)S(1)}, bf16[1040,128]{1,0:T(8,128)(2,1)S(1)}, f32[4,1,512]{2...) while((s32[]{:T(128)}, bf16[1552,128]{1,0:T(8,128)(2,1)S(1)}, ...), condition=%wide.region_2.3_spmd, body=%wide.region_1.2_spmd.sunk | while | flops 4296564736 | bytes 12730625 | solution.py:503
  60.7 1.8 %collective-permute-start.1 = (bf16[1568,128]{1,0:T(8,128)(2,1)S(1)}, bf16[1568,128]{1,0:T(8,128)(2,1)S(1)}, u32[]{:S(2)}, u32[]{:S(2)}) collective-permute-start(bf16[1568,128]{1,0:T(8,128)(2,1)S(1)} %pad_maximum_fusion.11), channel_id=1, source_target_pairs={{0,24},{8,0},{16,8},{24,16},{32,56},{40,32},{48,40},{56,48},{64,88... | collective-permute-start | bytes 1204232 | tf_op jit(solution)/shard_map/while/body/eval_jaxpr/ppermute | solution.py:44
  62.9 4.4 %attend_stage.13 = (f32[4,1,512]{2,1,0:T(1,128)S(1)}, f32[4,1,512]{2,1,0:T(1,128)S(1)}, f32[512,512]{1,0:T(8,128)}) custom-call(s32[1]{0:T(128)} %bitcast.65.number, s32[23]{0:T(128)S(1)} %get-tuple-element.483.info, bf16[512,512]{1,0:T(8,128)(2,1)S(1)} %get-tuple-element.484.queries, ...), custom_call_target="tpu_custom_call", output_to_operand_aliasing={{0}: (6, {}), {1}: (7, {}), {2}: (8, {})} | custom-call | flops 4294967296 | bytes 3145728 | tf_op jit(solution)/shard_map/while/body/eval_jaxpr/attend_stage/pallas_call | solution.py:310
  67.3 6.4 %collective-permute-done = bf16[1552,128]{1,0:T(8,128)(2,1)S(1)} collective-permute-done((bf16[1552,128]{1,0:T(8,128)(2,1)S(1)}, bf16[1552,128]{1,0:T(8,128)(2,1)S(1)}, u32[]{:S(2)}, u32[]{:S(2)}) %collective-permute-start) | collective-permute-done | bytes 397344 | tf_op jit(solution)/shard_map/while/body/eval_jaxpr/ppermute | solution.py:44
  74.0 3.0 %collective-permute-start.1 = (bf16[1568,128]{1,0:T(8,128)(2,1)S(1)}, bf16[1568,128]{1,0:T(8,128)(2,1)S(1)}, u32[]{:S(2)}, u32[]{:S(2)}) collective-permute-start(bf16[1568,128]{1,0:T(8,128)(2,1)S(1)} %pad_maximum_fusion.11), channel_id=1, source_target_pairs={{0,24},{8,0},{16,8},{24,16},{32,56},{40,32},{48,40},{56,48},{64,88... | collective-permute-start | bytes 1204232 | tf_op jit(solution)/shard_map/while/body/eval_jaxpr/ppermute | solution.py:44
  77.1 2.4 %attend_stage.13 = (f32[4,1,512]{2,1,0:T(1,128)S(1)}, f32[4,1,512]{2,1,0:T(1,128)S(1)}, f32[512,512]{1,0:T(8,128)}) custom-call(s32[1]{0:T(128)} %bitcast.65.number, s32[23]{0:T(128)S(1)} %get-tuple-element.483.info, bf16[512,512]{1,0:T(8,128)(2,1)S(1)} %get-tuple-element.484.queries, ...), custom_call_target="tpu_custom_call", output_to_operand_aliasing={{0}: (6, {}), {1}: (7, {}), {2}: (8, {})} | custom-call | flops 4294967296 | bytes 3145728 | tf_op jit(solution)/shard_map/while/body/eval_jaxpr/attend_stage/pallas_call | solution.py:310
  79.6 6.2 %collective-permute-done = bf16[1552,128]{1,0:T(8,128)(2,1)S(1)} collective-permute-done((bf16[1552,128]{1,0:T(8,128)(2,1)S(1)}, bf16[1552,128]{1,0:T(8,128)(2,1)S(1)}, u32[]{:S(2)}, u32[]{:S(2)}) %collective-permute-start) | collective-permute-done | bytes 397344 | tf_op jit(solution)/shard_map/while/body/eval_jaxpr/ppermute | solution.py:44
  85.9 1.1 collective-permute-start.2
  87.1 3.0 %collective-permute-start.1 = (bf16[1568,128]{1,0:T(8,128)(2,1)S(1)}, bf16[1568,128]{1,0:T(8,128)(2,1)S(1)}, u32[]{:S(2)}, u32[]{:S(2)}) collective-permute-start(bf16[1568,128]{1,0:T(8,128)(2,1)S(1)} %pad_maximum_fusion.11), channel_id=1, source_target_pairs={{0,24},{8,0},{16,8},{24,16},{32,56},{40,32},{48,40},{56,48},{64,88... | collective-permute-start | bytes 1204232 | tf_op jit(solution)/shard_map/while/body/eval_jaxpr/ppermute | solution.py:44
  90.3 2.4 %attend_stage.13 = (f32[4,1,512]{2,1,0:T(1,128)S(1)}, f32[4,1,512]{2,1,0:T(1,128)S(1)}, f32[512,512]{1,0:T(8,128)}) custom-call(s32[1]{0:T(128)} %bitcast.65.number, s32[23]{0:T(128)S(1)} %get-tuple-element.483.info, bf16[512,512]{1,0:T(8,128)(2,1)S(1)} %get-tuple-element.484.queries, ...), custom_call_target="tpu_custom_call", output_to_operand_aliasing={{0}: (6, {}), {1}: (7, {}), {2}: (8, {})} | custom-call | flops 4294967296 | bytes 3145728 | tf_op jit(solution)/shard_map/while/body/eval_jaxpr/attend_stage/pallas_call | solution.py:310
  92.7 5.4 %collective-permute-done = bf16[1552,128]{1,0:T(8,128)(2,1)S(1)} collective-permute-done((bf16[1552,128]{1,0:T(8,128)(2,1)S(1)}, bf16[1552,128]{1,0:T(8,128)(2,1)S(1)}, u32[]{:S(2)}, u32[]{:S(2)}) %collective-permute-start) | collective-permute-done | bytes 397344 | tf_op jit(solution)/shard_map/while/body/eval_jaxpr/ppermute | solution.py:44
  98.2 6.2 %collective-permute-start.2 = (bf16[1040,128]{1,0:T(8,128)(2,1)S(1)}, bf16[1040,128]{1,0:T(8,128)(2,1)S(1)}, u32[]{:S(2)}, u32[]{:S(2)}) collective-permute-start(bf16[1040,128]{1,0:T(8,128)(2,1)S(1)} %copy.25.refs_2_), channel_id=1, source_target_pairs={{0,32},{8,40},{16,48},{24,56},{32,64},{40,72},{48,80},{56,88},{64,... | collective-permute-start | bytes 798728 | tf_op jit(solution)/shard_map/while/body/eval_jaxpr/ppermute | solution.py:38
  104.5 3.3 %collective-permute-start.1 = (bf16[1568,128]{1,0:T(8,128)(2,1)S(1)}, bf16[1568,128]{1,0:T(8,128)(2,1)S(1)}, u32[]{:S(2)}, u32[]{:S(2)}) collective-permute-start(bf16[1568,128]{1,0:T(8,128)(2,1)S(1)} %pad_maximum_fusion.11), channel_id=1, source_target_pairs={{0,24},{8,0},{16,8},{24,16},{32,56},{40,32},{48,40},{56,48},{64,88... | collective-permute-start | bytes 1204232 | tf_op jit(solution)/shard_map/while/body/eval_jaxpr/ppermute | solution.py:44
  107.9 2.4 %attend_stage.13 = (f32[4,1,512]{2,1,0:T(1,128)S(1)}, f32[4,1,512]{2,1,0:T(1,128)S(1)}, f32[512,512]{1,0:T(8,128)}) custom-call(s32[1]{0:T(128)} %bitcast.65.number, s32[23]{0:T(128)S(1)} %get-tuple-element.483.info, bf16[512,512]{1,0:T(8,128)(2,1)S(1)} %get-tuple-element.484.queries, ...), custom_call_target="tpu_custom_call", output_to_operand_aliasing={{0}: (6, {}), {1}: (7, {}), {2}: (8, {})} | custom-call | flops 4294967296 | bytes 3145728 | tf_op jit(solution)/shard_map/while/body/eval_jaxpr/attend_stage/pallas_call | solution.py:310
  110.3 6.8 %collective-permute-done = bf16[1552,128]{1,0:T(8,128)(2,1)S(1)} collective-permute-done((bf16[1552,128]{1,0:T(8,128)(2,1)S(1)}, bf16[1552,128]{1,0:T(8,128)(2,1)S(1)}, u32[]{:S(2)}, u32[]{:S(2)}) %collective-permute-start) | collective-permute-done | bytes 397344 | tf_op jit(solution)/shard_map/while/body/eval_jaxpr/ppermute | solution.py:44
  117.2 1.3 collective-permute-start.14
  118.5 0.9 collective-permute-start.13
  119.4 2.4 %attend_stage.12 = (f32[4,1,512]{2,1,0:T(1,128)S(1)}, f32[4,1,512]{2,1,0:T(1,128)S(1)}, f32[512,512]{1,0:T(8,128)}) custom-call(s32[1]{0:T(128)} %constant.171.clone.1.number, s32[23]{0:T(128)S(1)} %get-tuple-element.523, bf16[512,512]{1,0:T(8,128)(2,1)S(1)} %get-tuple-element.533, ...), custom_call_target="tpu_custom_call", output_to_operand_aliasing={{0}: (5, {}), {1}: (6, {}), {2}: (7, {})} | custom-call | flops 3221225472 | bytes 3145728 | tf_op jit(solution)/shard_map/attend_stage/pallas_call | solution.py:310
  121.8 1.8 %collective-permute-done.13.keys = bf16[512,128]{1,0:T(8,128)(2,1)S(1)} collective-permute-done((bf16[512,128]{1,0:T(8,128)(2,1)S(1)}, bf16[512,128]{1,0:T(8,128)(2,1)S(1)}, u32[]{:S(2)}, u32[]{:S(2)}) %collective-permute-start.13) | collective-permute-done | bytes 131104 | tf_op jit(solution)/shard_map/ppermute | solution.py:44
  123.6 0.7 copy-done.12
  124.3 4.5 %finish.1 = (bf16[512,512]{1,0:T(8,128)(2,1)}, bf16[512,512]{1,0:T(8,128)(2,1)}, f32[512,512]{1,0:T(8,128)}) custom-call(s32[23]{0:T(128)S(1)} %get-tuple-element.523, s32[8]{0:T(128)} %get-tuple-element.325.columns, bf16[512,512]{1,0:T(8,128)(2,1)S(1)} %get-tuple-element.533, bf16[512,128]{1,0:T(8,128)(2,1)} %copy-done.12, bf16[528,128]{1,0:T(8,128)(2,1)} %copy-done.11, ...), custom_call_target="tpu_custom_call" | custom-call | flops 2147483648 | bytes 8388608 | tf_op jit(solution)/shard_map/finish/pallas_call | solution.py:380
  128.8 4.7 %three_products.3 = bf16[3,512,512]{2,1,0:T(8,128)(2,1)} custom-call(s32[8]{0:T(128)} %get-tuple-element.325.columns, bf16[512,512]{1,0:T(8,128)(2,1)} %get-tuple-element.354.heads, bf16[512,4096]{1,0:T(8,128)(2,1)} %weight.7), custom_call_target="tpu_custom_call" | custom-call | flops 1073741824 | bytes 6291456 | tf_op jit(solution)/shard_map/three_products/pallas_call | solution.py:420
  133.9 0.5 collective-permute-start.15
  134.4 3.9 %collective-permute-done.15 = bf16[512,512]{1,0:T(8,128)(2,1)S(1)} collective-permute-done((bf16[512,512]{1,0:T(8,128)(2,1)S(1)}, bf16[512,512]{1,0:T(8,128)(2,1)S(1)}, u32[]{:S(2)}, u32[]{:S(2)}) %collective-permute-start.15) | collective-permute-done | bytes 524320 | tf_op jit(solution)/shard_map/ppermute | solution.py:34
  138.5 3.2 %collective-permute-start.21 = (bf16[256,512]{1,0:T(8,128)(2,1)S(1)}, bf16[256,512]{1,0:T(8,128)(2,1)S(1)}, u32[]{:S(2)}, u32[]{:S(2)}) collective-permute-start(bf16[256,512]{1,0:T(8,128)(2,1)S(1)} %get-tuple-element.384), channel_id=1, source_target_pairs={{0,6},{2,0},{4,2},{6,4},{1,7},{3,1},{5,3},{7,5},{8,14},{10,8},{12,... | collective-permute-start | bytes 786440 | tf_op jit(solution)/shard_map/ppermute | solution.py:34
  141.8 5.1 %three_products.2 = f32[3,512,512]{2,1,0:T(8,128)} custom-call(s32[8]{0:T(128)} %get-tuple-element.325.columns, bf16[512,512]{1,0:T(8,128)(2,1)} %get-tuple-element.354.heads, bf16[512,4096]{1,0:T(8,128)(2,1)} %weight.7), custom_call_target="tpu_custom_call" | custom-call | flops 1073741824 | bytes 6291456 | tf_op jit(solution)/shard_map/three_products/pallas_call | solution.py:420
  146.8 1.2 collective-permute-done.17
  148.1 1.4 fusion.10
  149.6 3.2 %collective-permute-start.22 = (bf16[256,512]{1,0:T(8,128)(2,1)S(1)}, bf16[256,512]{1,0:T(8,128)(2,1)S(1)}, u32[]{:S(2)}, u32[]{:S(2)}) collective-permute-start(bf16[256,512]{1,0:T(8,128)(2,1)S(1)} %get-tuple-element.378), channel_id=1, source_target_pairs={{0,6},{2,0},{4,2},{6,4},{1,7},{3,1},{5,3},{7,5},{8,14},{10,8},{12,... | collective-permute-start | bytes 786440 | tf_op jit(solution)/shard_map/ppermute | solution.py:34
  152.8 1.4 fusion.14
  154.2 1.8 %collective-permute-start.19 = (bf16[256,512]{1,0:T(8,128)(2,1)S(1)}, bf16[256,512]{1,0:T(8,128)(2,1)S(1)}, u32[]{:S(2)}, u32[]{:S(2)}) collective-permute-start(bf16[256,512]{1,0:T(8,128)(2,1)S(1)} %get-tuple-element.379), channel_id=1, source_target_pairs={{0,6},{2,0},{4,2},{6,4},{1,7},{3,1},{5,3},{7,5},{8,14},{10,8},{12,... | collective-permute-start | bytes 786440 | tf_op jit(solution)/shard_map/ppermute | solution.py:34
  156.3 1.4 slice_add_fusion
  157.7 0.9 collective-permute-done.18
  158.6 0.9 collective-permute-done.22
  159.5 3.7 %collective-permute-done.19 = bf16[256,512]{1,0:T(8,128)(2,1)S(1)} collective-permute-done((bf16[256,512]{1,0:T(8,128)(2,1)S(1)}, bf16[256,512]{1,0:T(8,128)(2,1)S(1)}, u32[]{:S(2)}, u32[]{:S(2)}) %collective-permute-start.19) | collective-permute-done | bytes 262176 | tf_op jit(solution)/shard_map/ppermute | solution.py:34
  163.2 0.7 collective-permute-done.20
  164.1 0.8 pad_maximum_fusion.5
  (106 shorter events, 3.4 us)
Async XLA Ops:
  1.8 15.4 %copy-start.4 = (bf16[528,512]{1,0:T(8,128)(2,1)}, bf16[528,512]{1,0:T(8,128)(2,1)S(1)}, u32[]{:S(2)}) copy-start(bf16[528,512]{1,0:T(8,128)(2,1)S(1)} %pad_maximum_fusion.3.x0) | copy-start | bytes 1622020
  1.8 15.3 %collective-permute-start.3 = (bf16[528,512]{1,0:T(8,128)(2,1)S(1)}, bf16[528,512]{1,0:T(8,128)(2,1)S(1)}, u32[]{:S(2)}, u32[]{:S(2)}) collective-permute-start(bf16[528,512]{1,0:T(8,128)(2,1)S(1)} %pad_maximum_fusion.3.x0), channel_id=1, source_target_pairs={{0,2},{2,4},{4,6},{6,0},{1,3},{3,5},{5,7},{7,1},{8,10},{10,12},{12... | collective-permute-start | bytes 1622024 | tf_op jit(solution)/shard_map/ppermute | solution.py:34
  3.3 13.7 %collective-permute-start.4 = (bf16[528,512]{1,0:T(8,128)(2,1)S(1)}, bf16[528,512]{1,0:T(8,128)(2,1)S(1)}, u32[]{:S(2)}, u32[]{:S(2)}) collective-permute-start(bf16[528,512]{1,0:T(8,128)(2,1)S(1)} %pad_maximum_fusion.3.x0), channel_id=1, source_target_pairs={{0,6},{2,0},{4,2},{6,4},{1,7},{3,1},{5,3},{7,5},{8,14},{10,8},{12,... | collective-permute-start | bytes 1622024 | tf_op jit(solution)/shard_map/ppermute | solution.py:34
  5.1 12.0 %collective-permute-start.5 = (bf16[528,512]{1,0:T(8,128)(2,1)S(1)}, bf16[528,512]{1,0:T(8,128)(2,1)S(1)}, u32[]{:S(2)}, u32[]{:S(2)}) collective-permute-start(bf16[528,512]{1,0:T(8,128)(2,1)S(1)} %pad_maximum_fusion.3.x0), channel_id=1, source_target_pairs={{0,1},{1,0},{2,3},{3,2},{4,5},{5,4},{6,7},{7,6},{8,9},{9,8},{10,11... | collective-permute-start | bytes 1622024 | tf_op jit(solution)/shard_map/ppermute | solution.py:34
  17.1 3.3 %copy-start.2 = (bf16[528,512]{1,0:T(8,128)(2,1)}, bf16[528,512]{1,0:T(8,128)(2,1)S(1)}, u32[]{:S(2)}) copy-start(bf16[528,512]{1,0:T(8,128)(2,1)S(1)} %collective-permute-done.3.p0) | copy-start | bytes 1622020
  17.1 3.3 %copy-start.1 = (bf16[528,512]{1,0:T(8,128)(2,1)}, bf16[528,512]{1,0:T(8,128)(2,1)S(1)}, u32[]{:S(2)}) copy-start(bf16[528,512]{1,0:T(8,128)(2,1)S(1)} %collective-permute-done.4.m0) | copy-start | bytes 1622020
  17.1 3.3 %copy-start.8 = (bf16[528,512]{1,0:T(8,128)(2,1)}, bf16[528,512]{1,0:T(8,128)(2,1)S(1)}, u32[]{:S(2)}) copy-start(bf16[528,512]{1,0:T(8,128)(2,1)S(1)} %collective-permute-done.5.x1) | copy-start | bytes 1622020
  17.2 16.5 %collective-permute-start.8 = (bf16[1056,512]{1,0:T(8,128)(2,1)S(1)}, bf16[1056,512]{1,0:T(8,128)(2,1)S(1)}, u32[]{:S(2)}, u32[]{:S(2)}) collective-permute-start(bf16[1056,512]{1,0:T(8,128)(2,1)S(1)} %pad_maximum_fusion.2), channel_id=1, source_target_pairs={{0,1},{1,0},{2,3},{3,2},{4,5},{5,4},{6,7},{7,6},{8,9},{9,8},{10,11... | collective-permute-start | bytes 3244040 | tf_op jit(solution)/shard_map/ppermute | solution.py:34
  17.3 12.8 %collective-permute-start.7 = (bf16[272,512]{1,0:T(8,128)(2,1)S(1)}, bf16[272,512]{1,0:T(8,128)(2,1)S(1)}, u32[]{:S(2)}, u32[]{:S(2)}) collective-permute-start(bf16[272,512]{1,0:T(8,128)(2,1)S(1)} %slice.95), channel_id=1, source_target_pairs={{0,6},{2,0},{4,2},{6,4},{1,7},{3,1},{5,3},{7,5},{8,14},{10,8},{12,... | collective-permute-start | bytes 835592 | tf_op jit(solution)/shard_map/ppermute | solution.py:34
  20.4 9.7 %collective-permute-start.6 = (bf16[256,512]{1,0:T(8,128)(2,1)S(1)}, bf16[256,512]{1,0:T(8,128)(2,1)S(1)}, u32[]{:S(2)}, u32[]{:S(2)}) collective-permute-start(bf16[256,512]{1,0:T(8,128)(2,1)S(1)} %slice.94), channel_id=1, source_target_pairs={{0,2},{2,4},{4,6},{6,0},{1,3},{3,5},{5,7},{7,1},{8,10},{10,12},{12... | collective-permute-start | bytes 786440 | tf_op jit(solution)/shard_map/ppermute | solution.py:34
  30.1 3.6 %copy-start.6 = (bf16[256,512]{1,0:T(8,128)(2,1)}, bf16[256,512]{1,0:T(8,128)(2,1)S(1)}, u32[]{:S(2)}) copy-start(bf16[256,512]{1,0:T(8,128)(2,1)S(1)} %collective-permute-done.6.q0) | copy-start | bytes 786436
  30.1 3.6 %copy-start.5 = (bf16[272,512]{1,0:T(8,128)(2,1)}, bf16[272,512]{1,0:T(8,128)(2,1)S(1)}, u32[]{:S(2)}) copy-start(bf16[272,512]{1,0:T(8,128)(2,1)S(1)} %collective-permute-done.7.r0) | copy-start | bytes 835588
  31.6 2.0 %collective-permute-start.9 = (bf16[528,512]{1,0:T(8,128)(2,1)S(1)}, bf16[528,512]{1,0:T(8,128)(2,1)S(1)}, u32[]{:S(2)}, u32[]{:S(2)}) collective-permute-start(bf16[528,512]{1,0:T(8,128)(2,1)S(1)} %pad_maximum_fusion.4), channel_id=1, source_target_pairs={{0,1},{1,0},{2,3},{3,2},{4,5},{5,4},{6,7},{7,6},{8,9},{9,8},{10,11... | collective-permute-start | bytes 1622024 | tf_op jit(solution)/shard_map/ppermute | solution.py:34
  33.6 0.8 copy-start.9
  34.4 1.0 copy-start.7
  45.1 8.8 %collective-permute-start.11 = (bf16[1040,128]{1,0:T(8,128)(2,1)}, bf16[1040,128]{1,0:T(8,128)(2,1)S(1)}, u32[]{:S(2)}, u32[]{:S(2)}) collective-permute-start(bf16[1040,128]{1,0:T(8,128)(2,1)} %get-tuple-element.337.message), channel_id=1, source_target_pairs={{0,24},{8,0},{16,8},{24,16},{32,56},{40,32},{48,40},{56,48},{64,88... | collective-permute-start | bytes 798728 | tf_op jit(solution)/shard_map/ppermute | solution.py:44
  45.5 9.8 %collective-permute-start.10 = (bf16[1040,128]{1,0:T(8,128)(2,1)}, bf16[1040,128]{1,0:T(8,128)(2,1)S(1)}, u32[]{:S(2)}, u32[]{:S(2)}) collective-permute-start(bf16[1040,128]{1,0:T(8,128)(2,1)} %get-tuple-element.337.message), channel_id=1, source_target_pairs={{0,8},{8,16},{16,24},{24,0},{32,40},{40,48},{48,56},{56,32},{64,72... | collective-permute-start | bytes 798728 | tf_op jit(solution)/shard_map/ppermute | solution.py:44
  47.2 12.2 %collective-permute-start.12 = (bf16[1040,128]{1,0:T(8,128)(2,1)}, bf16[1040,128]{1,0:T(8,128)(2,1)S(1)}, u32[]{:S(2)}, u32[]{:S(2)}) collective-permute-start(bf16[1040,128]{1,0:T(8,128)(2,1)} %get-tuple-element.337.message), channel_id=1, source_target_pairs={{0,32},{8,40},{16,48},{24,56},{32,64},{40,72},{48,80},{56,88},{64,... | collective-permute-start | bytes 798728 | tf_op jit(solution)/shard_map/ppermute | solution.py:38
  60.5 2.4 %copy-start = (bf16[1040,128]{1,0:T(8,128)(2,1)}, bf16[1040,128]{1,0:T(8,128)(2,1)S(1)}, u32[]{:S(2)}) copy-start(bf16[1040,128]{1,0:T(8,128)(2,1)S(1)} %copy.25.refs_2_) | copy-start | bytes 798724 | tf_op jit(solution)/shard_map/while
  60.6 13.2 %collective-permute-start.2 = (bf16[1040,128]{1,0:T(8,128)(2,1)S(1)}, bf16[1040,128]{1,0:T(8,128)(2,1)S(1)}, u32[]{:S(2)}, u32[]{:S(2)}) collective-permute-start(bf16[1040,128]{1,0:T(8,128)(2,1)S(1)} %copy.25.refs_2_), channel_id=1, source_target_pairs={{0,32},{8,40},{16,48},{24,56},{32,64},{40,72},{48,80},{56,88},{64,... | collective-permute-start | bytes 798728 | tf_op jit(solution)/shard_map/while/body/eval_jaxpr/ppermute | solution.py:38
  60.7 13.0 %collective-permute-start.1 = (bf16[1568,128]{1,0:T(8,128)(2,1)S(1)}, bf16[1568,128]{1,0:T(8,128)(2,1)S(1)}, u32[]{:S(2)}, u32[]{:S(2)}) collective-permute-start(bf16[1568,128]{1,0:T(8,128)(2,1)S(1)} %pad_maximum_fusion.11), channel_id=1, source_target_pairs={{0,24},{8,0},{16,8},{24,16},{32,56},{40,32},{48,40},{56,48},{64,88... | collective-permute-start | bytes 1204232 | tf_op jit(solution)/shard_map/while/body/eval_jaxpr/ppermute | solution.py:44
  62.6 11.1 %collective-permute-start = (bf16[1552,128]{1,0:T(8,128)(2,1)S(1)}, bf16[1552,128]{1,0:T(8,128)(2,1)S(1)}, u32[]{:S(2)}, u32[]{:S(2)}) collective-permute-start(bf16[1552,128]{1,0:T(8,128)(2,1)S(1)} %pad_maximum_fusion.10), channel_id=1, source_target_pairs={{0,8},{8,16},{16,24},{24,0},{32,40},{40,48},{48,56},{56,32},{64,72... | collective-permute-start | bytes 1191944 | tf_op jit(solution)/shard_map/while/body/eval_jaxpr/ppermute | solution.py:44
  73.8 3.3 %copy-start = (bf16[1040,128]{1,0:T(8,128)(2,1)}, bf16[1040,128]{1,0:T(8,128)(2,1)S(1)}, u32[]{:S(2)}) copy-start(bf16[1040,128]{1,0:T(8,128)(2,1)S(1)} %copy.25.refs_2_) | copy-start | bytes 798724 | tf_op jit(solution)/shard_map/while
  73.8 12.1 %collective-permute-start.2 = (bf16[1040,128]{1,0:T(8,128)(2,1)S(1)}, bf16[1040,128]{1,0:T(8,128)(2,1)S(1)}, u32[]{:S(2)}, u32[]{:S(2)}) collective-permute-start(bf16[1040,128]{1,0:T(8,128)(2,1)S(1)} %copy.25.refs_2_), channel_id=1, source_target_pairs={{0,32},{8,40},{16,48},{24,56},{32,64},{40,72},{48,80},{56,88},{64,... | collective-permute-start | bytes 798728 | tf_op jit(solution)/shard_map/while/body/eval_jaxpr/ppermute | solution.py:38
  74.0 11.9 %collective-permute-start.1 = (bf16[1568,128]{1,0:T(8,128)(2,1)S(1)}, bf16[1568,128]{1,0:T(8,128)(2,1)S(1)}, u32[]{:S(2)}, u32[]{:S(2)}) collective-permute-start(bf16[1568,128]{1,0:T(8,128)(2,1)S(1)} %pad_maximum_fusion.11), channel_id=1, source_target_pairs={{0,24},{8,0},{16,8},{24,16},{32,56},{40,32},{48,40},{56,48},{64,88... | collective-permute-start | bytes 1204232 | tf_op jit(solution)/shard_map/while/body/eval_jaxpr/ppermute | solution.py:44
  77.0 8.8 %collective-permute-start = (bf16[1552,128]{1,0:T(8,128)(2,1)S(1)}, bf16[1552,128]{1,0:T(8,128)(2,1)S(1)}, u32[]{:S(2)}, u32[]{:S(2)}) collective-permute-start(bf16[1552,128]{1,0:T(8,128)(2,1)S(1)} %pad_maximum_fusion.10), channel_id=1, source_target_pairs={{0,8},{8,16},{16,24},{24,0},{32,40},{40,48},{48,56},{56,32},{64,72... | collective-permute-start | bytes 1191944 | tf_op jit(solution)/shard_map/while/body/eval_jaxpr/ppermute | solution.py:44
  85.9 4.3 %copy-start = (bf16[1040,128]{1,0:T(8,128)(2,1)}, bf16[1040,128]{1,0:T(8,128)(2,1)S(1)}, u32[]{:S(2)}) copy-start(bf16[1040,128]{1,0:T(8,128)(2,1)S(1)} %copy.25.refs_2_) | copy-start | bytes 798724 | tf_op jit(solution)/shard_map/while
  85.9 12.2 %collective-permute-start.2 = (bf16[1040,128]{1,0:T(8,128)(2,1)S(1)}, bf16[1040,128]{1,0:T(8,128)(2,1)S(1)}, u32[]{:S(2)}, u32[]{:S(2)}) collective-permute-start(bf16[1040,128]{1,0:T(8,128)(2,1)S(1)} %copy.25.refs_2_), channel_id=1, source_target_pairs={{0,32},{8,40},{16,48},{24,56},{32,64},{40,72},{48,80},{56,88},{64,... | collective-permute-start | bytes 798728 | tf_op jit(solution)/shard_map/while/body/eval_jaxpr/ppermute | solution.py:38
  87.1 11.0 %collective-permute-start.1 = (bf16[1568,128]{1,0:T(8,128)(2,1)S(1)}, bf16[1568,128]{1,0:T(8,128)(2,1)S(1)}, u32[]{:S(2)}, u32[]{:S(2)}) collective-permute-start(bf16[1568,128]{1,0:T(8,128)(2,1)S(1)} %pad_maximum_fusion.11), channel_id=1, source_target_pairs={{0,24},{8,0},{16,8},{24,16},{32,56},{40,32},{48,40},{56,48},{64,88... | collective-permute-start | bytes 1204232 | tf_op jit(solution)/shard_map/while/body/eval_jaxpr/ppermute | solution.py:44
  90.2 7.9 %collective-permute-start = (bf16[1552,128]{1,0:T(8,128)(2,1)S(1)}, bf16[1552,128]{1,0:T(8,128)(2,1)S(1)}, u32[]{:S(2)}, u32[]{:S(2)}) collective-permute-start(bf16[1552,128]{1,0:T(8,128)(2,1)S(1)} %pad_maximum_fusion.10), channel_id=1, source_target_pairs={{0,8},{8,16},{16,24},{24,0},{32,40},{40,48},{48,56},{56,32},{64,72... | collective-permute-start | bytes 1191944 | tf_op jit(solution)/shard_map/while/body/eval_jaxpr/ppermute | solution.py:44
  98.2 9.7 %copy-start = (bf16[1040,128]{1,0:T(8,128)(2,1)}, bf16[1040,128]{1,0:T(8,128)(2,1)S(1)}, u32[]{:S(2)}) copy-start(bf16[1040,128]{1,0:T(8,128)(2,1)S(1)} %copy.25.refs_2_) | copy-start | bytes 798724 | tf_op jit(solution)/shard_map/while
  98.2 18.9 %collective-permute-start.2 = (bf16[1040,128]{1,0:T(8,128)(2,1)S(1)}, bf16[1040,128]{1,0:T(8,128)(2,1)S(1)}, u32[]{:S(2)}, u32[]{:S(2)}) collective-permute-start(bf16[1040,128]{1,0:T(8,128)(2,1)S(1)} %copy.25.refs_2_), channel_id=1, source_target_pairs={{0,32},{8,40},{16,48},{24,56},{32,64},{40,72},{48,80},{56,88},{64,... | collective-permute-start | bytes 798728 | tf_op jit(solution)/shard_map/while/body/eval_jaxpr/ppermute | solution.py:38
  104.5 12.6 %collective-permute-start.1 = (bf16[1568,128]{1,0:T(8,128)(2,1)S(1)}, bf16[1568,128]{1,0:T(8,128)(2,1)S(1)}, u32[]{:S(2)}, u32[]{:S(2)}) collective-permute-start(bf16[1568,128]{1,0:T(8,128)(2,1)S(1)} %pad_maximum_fusion.11), channel_id=1, source_target_pairs={{0,24},{8,0},{16,8},{24,16},{32,56},{40,32},{48,40},{56,48},{64,88... | collective-permute-start | bytes 1204232 | tf_op jit(solution)/shard_map/while/body/eval_jaxpr/ppermute | solution.py:44
  107.8 9.3 %collective-permute-start = (bf16[1552,128]{1,0:T(8,128)(2,1)S(1)}, bf16[1552,128]{1,0:T(8,128)(2,1)S(1)}, u32[]{:S(2)}, u32[]{:S(2)}) collective-permute-start(bf16[1552,128]{1,0:T(8,128)(2,1)S(1)} %pad_maximum_fusion.10), channel_id=1, source_target_pairs={{0,8},{8,16},{16,24},{24,0},{32,40},{40,48},{48,56},{56,32},{64,72... | collective-permute-start | bytes 1191944 | tf_op jit(solution)/shard_map/while/body/eval_jaxpr/ppermute | solution.py:44
  117.2 6.4 %collective-permute-start.14 = (bf16[528,128]{1,0:T(8,128)(2,1)S(1)}, bf16[528,128]{1,0:T(8,128)(2,1)S(1)}, u32[]{:S(2)}, u32[]{:S(2)}) collective-permute-start(bf16[528,128]{1,0:T(8,128)(2,1)S(1)} %slice.97), channel_id=1, source_target_pairs={{0,24},{8,0},{16,8},{24,16},{32,56},{40,32},{48,40},{56,48},{64,88... | collective-permute-start | bytes 405512 | tf_op jit(solution)/shard_map/ppermute | solution.py:44
  118.5 5.0 %collective-permute-start.13 = (bf16[512,128]{1,0:T(8,128)(2,1)S(1)}, bf16[512,128]{1,0:T(8,128)(2,1)S(1)}, u32[]{:S(2)}, u32[]{:S(2)}) collective-permute-start(bf16[512,128]{1,0:T(8,128)(2,1)S(1)} %slice.96), channel_id=1, source_target_pairs={{0,8},{8,16},{16,24},{24,0},{32,40},{40,48},{48,56},{56,32},{64,72... | collective-permute-start | bytes 393224 | tf_op jit(solution)/shard_map/ppermute | solution.py:44
  123.6 0.7 copy-start.12
  123.6 0.7 copy-start.11
  128.8 5.1 %copy-start.10 = (bf16[512,512]{1,0:T(8,128)(2,1)S(1)}, bf16[512,512]{1,0:T(8,128)(2,1)}, u32[]{:S(2)}) copy-start(bf16[512,512]{1,0:T(8,128)(2,1)} %get-tuple-element.353) | copy-start | bytes 1572868
  128.8 9.4 %copy-start.3 = (f32[512,512]{1,0:T(8,128)S(1)}, f32[512,512]{1,0:T(8,128)}, u32[]{:S(2)}) copy-start(f32[512,512]{1,0:T(8,128)} %get-tuple-element.352) | copy-start | bytes 3145732
  133.6 14.5 %collective-permute-start.16 = (bf16[3,512,512]{2,1,0:T(8,128)(2,1)}, bf16[3,512,512]{2,1,0:T(8,128)(2,1)S(1)}, u32[]{:S(2)}, u32[]{:S(2)}) collective-permute-start(bf16[3,512,512]{2,1,0:T(8,128)(2,1)} %three_products.3), channel_id=1, source_target_pairs={{0,1},{1,0},{2,3},{3,2},{4,5},{5,4},{6,7},{7,6},{8,9},{9,8},{10,11... | collective-permute-start | bytes 4718600 | tf_op jit(solution)/shard_map/ppermute | solution.py:34
  133.9 4.3 %collective-permute-start.15 = (bf16[512,512]{1,0:T(8,128)(2,1)S(1)}, bf16[512,512]{1,0:T(8,128)(2,1)S(1)}, u32[]{:S(2)}, u32[]{:S(2)}) collective-permute-start(bf16[512,512]{1,0:T(8,128)(2,1)S(1)} %copy-done.10), channel_id=1, source_target_pairs={{0,1},{1,0},{2,3},{3,2},{4,5},{5,4},{6,7},{7,6},{8,9},{9,8},{10,11... | collective-permute-start | bytes 1572872 | tf_op jit(solution)/shard_map/ppermute | solution.py:34
  138.4 9.6 %collective-permute-start.17 = (bf16[256,512]{1,0:T(8,128)(2,1)S(1)}, bf16[256,512]{1,0:T(8,128)(2,1)S(1)}, u32[]{:S(2)}, u32[]{:S(2)}) collective-permute-start(bf16[256,512]{1,0:T(8,128)(2,1)S(1)} %get-tuple-element.383), channel_id=1, source_target_pairs={{0,2},{2,4},{4,6},{6,0},{1,3},{3,5},{5,7},{7,1},{8,10},{10,12},{12... | collective-permute-start | bytes 786440 | tf_op jit(solution)/shard_map/ppermute | solution.py:34
  138.5 9.5 %collective-permute-start.21 = (bf16[256,512]{1,0:T(8,128)(2,1)S(1)}, bf16[256,512]{1,0:T(8,128)(2,1)S(1)}, u32[]{:S(2)}, u32[]{:S(2)}) collective-permute-start(bf16[256,512]{1,0:T(8,128)(2,1)S(1)} %get-tuple-element.384), channel_id=1, source_target_pairs={{0,6},{2,0},{4,2},{6,4},{1,7},{3,1},{5,3},{7,5},{8,14},{10,8},{12,... | collective-permute-start | bytes 786440 | tf_op jit(solution)/shard_map/ppermute | solution.py:34
  149.5 9.1 %collective-permute-start.18 = (bf16[256,512]{1,0:T(8,128)(2,1)S(1)}, bf16[256,512]{1,0:T(8,128)(2,1)S(1)}, u32[]{:S(2)}, u32[]{:S(2)}) collective-permute-start(bf16[256,512]{1,0:T(8,128)(2,1)S(1)} %get-tuple-element.377), channel_id=1, source_target_pairs={{0,2},{2,4},{4,6},{6,0},{1,3},{3,5},{5,7},{7,1},{8,10},{10,12},{12... | collective-permute-start | bytes 786440 | tf_op jit(solution)/shard_map/ppermute | solution.py:34
  149.6 9.9 %collective-permute-start.22 = (bf16[256,512]{1,0:T(8,128)(2,1)S(1)}, bf16[256,512]{1,0:T(8,128)(2,1)S(1)}, u32[]{:S(2)}, u32[]{:S(2)}) collective-permute-start(bf16[256,512]{1,0:T(8,128)(2,1)S(1)} %get-tuple-element.378), channel_id=1, source_target_pairs={{0,6},{2,0},{4,2},{6,4},{1,7},{3,1},{5,3},{7,5},{8,14},{10,8},{12,... | collective-permute-start | bytes 786440 | tf_op jit(solution)/shard_map/ppermute | solution.py:34
  154.2 9.0 %collective-permute-start.19 = (bf16[256,512]{1,0:T(8,128)(2,1)S(1)}, bf16[256,512]{1,0:T(8,128)(2,1)S(1)}, u32[]{:S(2)}, u32[]{:S(2)}) collective-permute-start(bf16[256,512]{1,0:T(8,128)(2,1)S(1)} %get-tuple-element.379), channel_id=1, source_target_pairs={{0,6},{2,0},{4,2},{6,4},{1,7},{3,1},{5,3},{7,5},{8,14},{10,8},{12,... | collective-permute-start | bytes 786440 | tf_op jit(solution)/shard_map/ppermute | solution.py:34
  156.0 7.9 %collective-permute-start.20 = (bf16[256,512]{1,0:T(8,128)(2,1)S(1)}, bf16[256,512]{1,0:T(8,128)(2,1)S(1)}, u32[]{:S(2)}, u32[]{:S(2)}) collective-permute-start(bf16[256,512]{1,0:T(8,128)(2,1)S(1)} %get-tuple-element.380), channel_id=1, source_target_pairs={{0,2},{2,4},{4,6},{6,0},{1,3},{3,5},{5,7},{7,1},{8,10},{10,12},{12... | collective-permute-start | bytes 786440 | tf_op jit(solution)/shard_map/ppermute | solution.py:34

commit v2 on v1

--- a/solution.py
+++ b/solution.py
@@ -261,8 +261,10 @@
 
 
 def attend_first(queries, message, doc_rows, doc_columns):
-    def kernel(message, queries, doc_rows, doc_columns, *state):
+    def kernel(message, queries, doc_rows, doc_columns, *states):
+        state = states[:3]
         clear(*state)
+        clear(*states[3:])
 
         def change(scores, at):
             key = lax.broadcasted_iota(jnp.int32, scores.shape, 0)
@@ -272,17 +274,18 @@
 
         attend_block(message, queries, *state, change, 1)
 
-    return pl.pallas_call(
+    made = pl.pallas_call(
         kernel,
-        out_shape=STATE,
+        out_shape=STATE + STATE,
         in_specs=vmem(4),
-        out_specs=tuple(vmem(3)),
+        out_specs=tuple(vmem(6)),
         compiler_params=params(),
         cost_estimate=pl.CostEstimate(
             flops=2 * BLOCK_FLOPS, transcendentals=GROUP * T * T, bytes_accessed=2 << 20
         ),
         name="attend_own",
     )(message, queries, doc_rows, doc_columns)
+    return made[:3], made[3:]
 
 
 def attend_stage(number, info, queries, state, along, against, straight):
@@ -348,9 +351,9 @@
     def kernel(
         info, columns, queries, keys, values, own_highest, own_totals, own_accum,
         old_highest, old_totals, old_accum, weight,
-        heads, first, far, highest, totals, accum, blocks, bias, sems, held, held_sems,
+        first, others, products, highest, totals, accum, blocks, bias, sems, held, held_sems, heads,
     ):
-        fetches = fetch_columns(columns, 0, 2, weight, held, held_sems)
+        fetches = fetch_columns(columns, 0, 8, weight, held, held_sems)
 
         def fill():
             highest[...] = old_highest[...]
@@ -374,15 +377,29 @@
             heads[:, rows] = (summed / total).astype(bf16).T
         for fetch in fetches:
             fetch.wait()
-        first[...] = jnp.dot(heads[...], held[0], preferred_element_type=f32).astype(bf16)
-        far[...] = jnp.dot(heads[...], held[1], preferred_element_type=f32)
+
+        def product(k):
+            return jnp.dot(heads[...], held[k], preferred_element_type=f32)
+
+        first[...] = product(0).astype(bf16)
+
+        def partner(k, _):
+            others[k] = product(1 + k).astype(bf16)
+            return 0
+
+        def kept(k, _):
+            products[k] = product(4 + k)
+            return 0
+
+        lax.fori_loop(0, 3, partner, 0)
+        lax.fori_loop(0, 4, kept, 0)
 
     return pl.pallas_call(
         kernel,
         out_shape=(
-            jax.ShapeDtypeStruct((T, GROUP * HEAD_SIZE), bf16),
             jax.ShapeDtypeStruct((T, PIECE), bf16),
-            jax.ShapeDtypeStruct((T, PIECE), f32),
+            jax.ShapeDtypeStruct((3, T, PIECE), bf16),
+            jax.ShapeDtypeStruct((4, T, PIECE), f32),
         ),
         in_specs=[smem(), smem()]
         + vmem(1)
@@ -396,39 +413,14 @@
             pltpu.VMEM((GROUP * HEAD_SIZE, T), f32),
         ]
         + earlier_scratch(1)
-        + column_scratch(2),
+        + column_scratch(8)
+        + [pltpu.VMEM((T, GROUP * HEAD_SIZE), bf16)],
         compiler_params=params(),
         cost_estimate=pl.CostEstimate(
             flops=2 * T * T * MODEL_WIDTH, transcendentals=0, bytes_accessed=8 << 20
         ),
         name="finish",
     )(info, columns, queries, keys, values, *own_state, *state, weight)
-
-
-def three_products(columns, start, heads, weight, dtype):
-    def kernel(columns, heads, weight, out, held, sems):
-        fetches = fetch_columns(columns, start, 3, weight, held, sems)
-
-        def multiply(k, _):
-            for j in range(3):
-                pl.when(k == j)(fetches[j].wait)
-            out[k] = jnp.dot(heads[...], held[k], preferred_element_type=f32).astype(dtype)
-            return 0
-
-        lax.fori_loop(0, 3, multiply, 0)
-
-    return pl.pallas_call(
-        kernel,
-        out_shape=jax.ShapeDtypeStruct((3, T, PIECE), dtype),
-        in_specs=[smem()] + vmem(1) + [pl.BlockSpec(memory_space=pl.ANY)],
-        out_specs=vmem(1)[0],
-        scratch_shapes=column_scratch(3),
-        compiler_params=params(),
-        cost_estimate=pl.CostEstimate(
-            flops=2 * T * T * MODEL_WIDTH // 2, transcendentals=0, bytes_accessed=6 << 20
-        ),
-        name="three_products",
-    )(columns, heads, weight)
 
 
 def body(tokens, norm_gain, query_key_value_weight, out_weight, doc_ids):
@@ -462,32 +454,22 @@
         [shard, doc_ids[0], jnp.sum((doc_ids == doc_ids[0]).astype(jnp.int32))] + blocks
     ).astype(jnp.int32)
     order = jnp.stack([(chip + 2) % 4, (chip + 1) % 4, (chip + 3) % 4, chip])
-    columns = jnp.concatenate(
-        [order[:1] * 2 + 1 - core, order[:1] * 2 + core, order[1:] * 2 + 1 - core, order[1:] * 2 + core]
-    ).astype(jnp.int32)
-
-    behind, ahead, across, fids, info, columns, cosine, sine, ids = lax.optimization_barrier(
-        (behind, ahead, across, fids, info, columns, cosine, sine, ids)
-    )
+    columns = jnp.concatenate([order * 2 + 1 - core, order * 2 + core]).astype(jnp.int32)
+
+    tables = (fids, info, columns, cosine, sine, ids, doc_rows, doc_columns)
+    behind, ahead, across, tables = lax.optimization_barrier((behind, ahead, across, tables))
+    fids, info, columns, cosine, sine, ids, doc_rows, doc_columns = tables
     top = shift(behind[:HALF], "head", 1)
     bottom = shift(ahead[HALF:], "head", -1)
     across_near = shift(jnp.concatenate([behind, ahead]), "grp", 1)
-    top, bottom, doc_rows, doc_columns = lax.optimization_barrier(
-        (top, bottom, doc_rows, doc_columns)
-    )
     mine = [own, behind, ahead, top, bottom]
     across_far = shift(jnp.concatenate([top, bottom]), "grp", 1)
     theirs = [across, across_near, across_far]
     queries, message = project(fids, mine + theirs, query_key_value_weight, cosine, sine, ids)
 
-    state = (
-        jnp.full((GROUP, 1, T), floor_score, f32),
-        jnp.zeros((GROUP, 1, T), f32),
-        jnp.zeros((GROUP * HEAD_SIZE, T), f32),
-    )
     along, against = shift_y(message, 1), shift_y(message, -1)
     straight = shift_z(message)
-    own_state = attend_first(queries, message, doc_rows, doc_columns)
+    own_state, state = attend_first(queries, message, doc_rows, doc_columns)
     along = jnp.pad(along, ((0, T), (0, 0)))
     against = jnp.pad(against, ((0, MSG_ROWS - T), (0, 0)))
 
@@ -509,27 +491,24 @@
         jnp.full((1,), 4, jnp.int32), info, queries, state, along, against, None
     )
 
-    heads, first, products = finish(
+    first, others, products = finish(
         info, queries, own_state, state, keys, values, columns, out_weight
     )
     first = shift(first, "grp", 1)
-    others = three_products(columns, 2, heads, out_weight, bf16)
     others = shift(others, "grp", 1)
 
-    far = (products + first.astype(f32)).astype(bf16)
+    far = (products[0] + first.astype(f32)).astype(bf16)
     far_up = shift(far[:HALF], "head", 1)
     far_down = shift(far[HALF:], "head", -1)
-    heads, far = lax.optimization_barrier((heads, far))
-    products = three_products(columns, 5, heads, out_weight, f32)
-    up_low = (products[0, HALF:] + others[0, HALF:].astype(f32)).astype(bf16)
-    down_high = (products[1, :HALF] + others[1, :HALF].astype(f32)).astype(bf16)
+    up_low = (products[1, HALF:] + others[0, HALF:].astype(f32)).astype(bf16)
+    down_high = (products[2, :HALF] + others[1, :HALF].astype(f32)).astype(bf16)
     up_low = shift(up_low, "head", 1)
     down_high = shift(down_high, "head", -1)
-    up_high = products[0, :HALF] + others[0, :HALF].astype(f32) + far_up.astype(f32)
-    down_low = products[1, HALF:] + others[1, HALF:].astype(f32) + far_down.astype(f32)
+    up_high = products[1, :HALF] + others[0, :HALF].astype(f32) + far_up.astype(f32)
+    down_low = products[2, HALF:] + others[1, HALF:].astype(f32) + far_down.astype(f32)
     up_high = shift(up_high.astype(bf16), "head", 1)
     down_low = shift(down_low.astype(bf16), "head", -1)
-    kept = products[2] + others[2].astype(f32)
+    kept = products[3] + others[2].astype(f32)
     return jnp.concatenate(
         [
             kept[:HALF] + up_high.astype(f32) + down_high.astype(f32),

time: 168 us -> 168 us (level)
  the two profiles are of different devices: /device:TPU:8 before, /device:TPU:134 now
where the time goes in v2:
time: 168 us; the launch traced here: 167 us
  Pallas kernels  65.7 us (39%)
  waiting for transfers between devices  40.6 us (24%)
  starting transfers between devices  40.4 us (24%)
  other arithmetic  11.1 us (7%)
  local copies, waits for them, and re-layouts  8.49 us (5%)
    pallas_call x5, Pallas kernels, attend_stage(): pl.pallas_call(kernel, out_shape=STATE, in_specs=[smem(), smem()] + vmem(...  41.1 us
    ppermute x15, waiting for transfers between devices, shift(): return lax.ppermute(x, axis, [(i, (i + distance) % n) for i in range(n)])  34.6 us
    ppermute x12, starting transfers between devices, shift_y(): lax.ppermute(x, 'tok', [(z * Y + y, z * Y + (y + distance) % Y) for z in...  21 us
    ppermute x15, starting transfers between devices, shift(): return lax.ppermute(x, axis, [(i, (i + distance) % n) for i in range(n)])  16 us
    pallas_call x1, Pallas kernels, finish(): pl.pallas_call(kernel, out_shape=(jax.ShapeDtypeStruct((T, PIECE), bf16),...  10.1 us
    pallas_call x1, Pallas kernels, project(): pl.pallas_call(project_kernel, out_shape=(jax.ShapeDtypeStruct((GROUP * H...  9.61 us
    ppermute x12, waiting for transfers between devices, shift_y(): lax.ppermute(x, 'tok', [(z * Y + y, z * Y + (y + distance) % Y) for z in...  5.97 us
    pallas_call x1, Pallas kernels, attend_first(): pl.pallas_call(kernel, out_shape=STATE + STATE, in_specs=vmem(4), out_spe...  4.88 us
  transfers between devices with their start and end apart: 32, of which 13 were waited for; matrix products, arithmetic and copies ran while one was open for 7% of the time, Pallas kernels for 28%

profile of v2, /device:TPU:134, one launch (start us, length us, event | category | flops | bytes accessed | tf_op | source)
XLA Modules:
  0.0 167.0 jit_solution(5349624683844630336)
XLA Ops:
  0.0 0.7 broadcast_in_dim.8
  0.7 1.1 pad_maximum_fusion.3.x0
  1.8 0.1 collective-permute-start.5
  1.9 0.9 collective-permute-start.4
  2.8 2.4 %collective-permute-start.3 = (bf16[528,512]{1,0:T(8,128)(2,1)S(1)}, bf16[528,512]{1,0:T(8,128)(2,1)S(1)}, u32[]{:S(2)}, u32[]{:S(2)}) collective-permute-start(bf16[528,512]{1,0:T(8,128)(2,1)S(1)} %pad_maximum_fusion.3.x0), channel_id=1, source_target_pairs={{0,2},{2,4},{4,6},{6,0},{1,3},{3,5},{5,7},{7,1},{8,10},{10,12},{12... | collective-permute-start | bytes 1622024 | tf_op jit(solution)/shard_map/ppermute | solution.py:34
  5.2 1.3 slice.93
  6.5 2.1 %fusion.13 = (f32[512]{0:T(512)S(1)}, s32[]{:T(128)}, bf16[4,128]{1,0:T(4,128)(2,1)S(1)}) fusion(s32[512]{0:T(512)} %param.11, s32[]{:T(128)} %bitcast.6), kind=kLoop, calls=%fused_computation.43 | loop fusion | flops 2559 | bytes 5128 | tf_op jit(solution)/shard_map/convert_element_type | solution.py:449
  8.6 0.6 pad_add_fusion.fids
  9.2 0.6 concatenate.59.ids
  9.8 1.4 stack.120.info
  11.2 0.6 pad_add_fusion.1.columns
  11.8 1.0 fusion.11
  12.8 1.0 pad_maximum_fusion.6
  13.8 4.0 %collective-permute-done.4.m0 = bf16[528,512]{1,0:T(8,128)(2,1)S(1)} collective-permute-done((bf16[528,512]{1,0:T(8,128)(2,1)S(1)}, bf16[528,512]{1,0:T(8,128)(2,1)S(1)}, u32[]{:S(2)}, u32[]{:S(2)}) %collective-permute-start.4) | collective-permute-done | bytes 540704 | tf_op jit(solution)/shard_map/ppermute | solution.py:34
  17.8 0.7 broadcast_in_dim.10.doc_columns
  18.4 0.9 broadcast_in_dim.9.doc_rows
  19.4 0.1 collective-permute-start.8
  19.6 3.3 %collective-permute-start.6 = (bf16[256,512]{1,0:T(8,128)(2,1)S(1)}, bf16[256,512]{1,0:T(8,128)(2,1)S(1)}, u32[]{:S(2)}, u32[]{:S(2)}) collective-permute-start(bf16[256,512]{1,0:T(8,128)(2,1)S(1)} %slice.94), channel_id=1, source_target_pairs={{0,2},{2,4},{4,6},{6,0},{1,3},{3,5},{5,7},{7,1},{8,10},{10,12},{12... | collective-permute-start | bytes 786440 | tf_op jit(solution)/shard_map/ppermute | solution.py:34
  22.9 5.9 %collective-permute-done.6.q0 = bf16[256,512]{1,0:T(8,128)(2,1)S(1)} collective-permute-done((bf16[256,512]{1,0:T(8,128)(2,1)S(1)}, bf16[256,512]{1,0:T(8,128)(2,1)S(1)}, u32[]{:S(2)}, u32[]{:S(2)}) %collective-permute-start.6) | collective-permute-done | bytes 262176 | tf_op jit(solution)/shard_map/ppermute | solution.py:34
  28.9 1.0 collective-permute-done.7.r0
  30.0 1.9 %collective-permute-done.9.qr1 = bf16[528,512]{1,0:T(8,128)(2,1)S(1)} collective-permute-done((bf16[528,512]{1,0:T(8,128)(2,1)S(1)}, bf16[528,512]{1,0:T(8,128)(2,1)S(1)}, u32[]{:S(2)}, u32[]{:S(2)}) %collective-permute-start.9) | collective-permute-done | bytes 540704 | tf_op jit(solution)/shard_map/ppermute | solution.py:34
  31.9 0.8 copy-done.9
  32.7 1.0 copy-done.7
  33.7 9.6 %project.1 = (bf16[512,512]{1,0:T(8,128)(2,1)S(1)}, bf16[1040,128]{1,0:T(8,128)(2,1)}) custom-call(s32[8]{0:T(128)} %pad_add_fusion.fids, bf16[528,512]{1,0:T(8,128)(2,1)} %copy-done.4, bf16[528,512]{1,0:T(8,128)(2,1)} %copy-done.3, bf16[528,512]{1,0:T(8,128)(2,1)} %copy-done.2, bf16[256,512]{1,0:T(8,128)(2,1)} %copy-done.6, bf16[272,512]{1,0:T(8,128)(2,1)} %copy-done.5, ...), custom_call_target="tpu_custom_call" | custom-call | flops 3221225472 | bytes 12582912 | tf_op jit(solution)/shard_map/project/pallas_call | solution.py:126
  43.3 3.1 %collective-permute-start.11 = (bf16[1040,128]{1,0:T(8,128)(2,1)}, bf16[1040,128]{1,0:T(8,128)(2,1)S(1)}, u32[]{:S(2)}, u32[]{:S(2)}) collective-permute-start(bf16[1040,128]{1,0:T(8,128)(2,1)} %get-tuple-element.335.message), channel_id=1, source_target_pairs={{0,24},{8,0},{16,8},{24,16},{32,56},{40,32},{48,40},{56,48},{64,88... | collective-permute-start | bytes 798728 | tf_op jit(solution)/shard_map/ppermute | solution.py:44
  46.4 1.0 collective-permute-start.12
  47.4 4.9 %attend_own.1 = (f32[4,1,512]{2,1,0:T(1,128)}, f32[4,1,512]{2,1,0:T(1,128)}, f32[512,512]{1,0:T(8,128)}, f32[4,1,512]{2,1,0:T(1,128)S(1)}, f32[4,1,512]{2,1,0:T(1,128)S(1)}, /*index=5*/f32[512,512]{1,0:T(8,128)}) custom-call(bf16[1040,128]{1,0:T(8,128)(2,1)} %get-tuple-element.335.message, bf16[512,512]{1,0:T(8,128)(2,1)S(1)} %get-tuple-element.464.queries, ...), custom_call_target="tpu_custom_call" | custom-call | flops 1073741824 | bytes 2097152 | tf_op jit(solution)/shard_map/attend_own/pallas_call | solution.py:277
  52.3 0.4 collective-permute-done.11
  52.7 3.3 %collective-permute-done.10 = bf16[1040,128]{1,0:T(8,128)(2,1)S(1)} collective-permute-done((bf16[1040,128]{1,0:T(8,128)(2,1)}, bf16[1040,128]{1,0:T(8,128)(2,1)S(1)}, u32[]{:S(2)}, u32[]{:S(2)}) %collective-permute-start.10) | collective-permute-done | bytes 266272 | tf_op jit(solution)/shard_map/ppermute | solution.py:44
  56.0 54.5 %while.27 = (s32[]{:T(128)}, bf16[1552,128]{1,0:T(8,128)(2,1)S(1)}, bf16[1568,128]{1,0:T(8,128)(2,1)S(1)}, bf16[1040,128]{1,0:T(8,128)(2,1)S(1)}, f32[4,1,512]{2...) while((s32[]{:T(128)}, bf16[1552,128]{1,0:T(8,128)(2,1)S(1)}, ...), condition=%wide.region_2.3_spmd, body=%wide.region_1.2_spmd.sunk | while | flops 4296564736 | bytes 12730625 | solution.py:485
  56.1 1.1 collective-permute-start.2
  57.4 3.3 %collective-permute-start.1 = (bf16[1568,128]{1,0:T(8,128)(2,1)S(1)}, bf16[1568,128]{1,0:T(8,128)(2,1)S(1)}, u32[]{:S(2)}, u32[]{:S(2)}) collective-permute-start(bf16[1568,128]{1,0:T(8,128)(2,1)S(1)} %pad_maximum_fusion.11), channel_id=1, source_target_pairs={{0,24},{8,0},{16,8},{24,16},{32,56},{40,32},{48,40},{56,48},{64,88... | collective-permute-start | bytes 1204232 | tf_op jit(solution)/shard_map/while/body/eval_jaxpr/ppermute | solution.py:44
  60.7 5.4 %attend_stage.13 = (f32[4,1,512]{2,1,0:T(1,128)S(1)}, f32[4,1,512]{2,1,0:T(1,128)S(1)}, f32[512,512]{1,0:T(8,128)}) custom-call(s32[1]{0:T(128)} %bitcast.64.number, s32[23]{0:T(128)S(1)} %get-tuple-element.483.info, bf16[512,512]{1,0:T(8,128)(2,1)S(1)} %get-tuple-element.484.queries, ...), custom_call_target="tpu_custom_call", output_to_operand_aliasing={{0}: (6, {}), {1}: (7, {}), {2}: (8, {})} | custom-call | flops 4294967296 | bytes 3145728 | tf_op jit(solution)/shard_map/while/body/eval_jaxpr/attend_stage/pallas_call | solution.py:313
  66.1 2.3 %collective-permute-done = bf16[1552,128]{1,0:T(8,128)(2,1)S(1)} collective-permute-done((bf16[1552,128]{1,0:T(8,128)(2,1)S(1)}, bf16[1552,128]{1,0:T(8,128)(2,1)S(1)}, u32[]{:S(2)}, u32[]{:S(2)}) %collective-permute-start) | collective-permute-done | bytes 397344 | tf_op jit(solution)/shard_map/while/body/eval_jaxpr/ppermute | solution.py:44
  68.5 1.1 collective-permute-start.2
  69.8 3.3 %collective-permute-start.1 = (bf16[1568,128]{1,0:T(8,128)(2,1)S(1)}, bf16[1568,128]{1,0:T(8,128)(2,1)S(1)}, u32[]{:S(2)}, u32[]{:S(2)}) collective-permute-start(bf16[1568,128]{1,0:T(8,128)(2,1)S(1)} %pad_maximum_fusion.11), channel_id=1, source_target_pairs={{0,24},{8,0},{16,8},{24,16},{32,56},{40,32},{48,40},{56,48},{64,88... | collective-permute-start | bytes 1204232 | tf_op jit(solution)/shard_map/while/body/eval_jaxpr/ppermute | solution.py:44
  73.1 8.6 %attend_stage.13 = (f32[4,1,512]{2,1,0:T(1,128)S(1)}, f32[4,1,512]{2,1,0:T(1,128)S(1)}, f32[512,512]{1,0:T(8,128)}) custom-call(s32[1]{0:T(128)} %bitcast.64.number, s32[23]{0:T(128)S(1)} %get-tuple-element.483.info, bf16[512,512]{1,0:T(8,128)(2,1)S(1)} %get-tuple-element.484.queries, ...), custom_call_target="tpu_custom_call", output_to_operand_aliasing={{0}: (6, {}), {1}: (7, {}), {2}: (8, {})} | custom-call | flops 4294967296 | bytes 3145728 | tf_op jit(solution)/shard_map/while/body/eval_jaxpr/attend_stage/pallas_call | solution.py:313
  82.0 0.2 collective-permute-start
  82.2 4.3 %collective-permute-start.1 = (bf16[1568,128]{1,0:T(8,128)(2,1)S(1)}, bf16[1568,128]{1,0:T(8,128)(2,1)S(1)}, u32[]{:S(2)}, u32[]{:S(2)}) collective-permute-start(bf16[1568,128]{1,0:T(8,128)(2,1)S(1)} %pad_maximum_fusion.11), channel_id=1, source_target_pairs={{0,24},{8,0},{16,8},{24,16},{32,56},{40,32},{48,40},{56,48},{64,88... | collective-permute-start | bytes 1204232 | tf_op jit(solution)/shard_map/while/body/eval_jaxpr/ppermute | solution.py:44
  86.6 11.0 %attend_stage.13 = (f32[4,1,512]{2,1,0:T(1,128)S(1)}, f32[4,1,512]{2,1,0:T(1,128)S(1)}, f32[512,512]{1,0:T(8,128)}) custom-call(s32[1]{0:T(128)} %bitcast.64.number, s32[23]{0:T(128)S(1)} %get-tuple-element.483.info, bf16[512,512]{1,0:T(8,128)(2,1)S(1)} %get-tuple-element.484.queries, ...), custom_call_target="tpu_custom_call", output_to_operand_aliasing={{0}: (6, {}), {1}: (7, {}), {2}: (8, {})} | custom-call | flops 4294967296 | bytes 3145728 | tf_op jit(solution)/shard_map/while/body/eval_jaxpr/attend_stage/pallas_call | solution.py:313
  98.0 3.3 %collective-permute-start.1 = (bf16[1568,128]{1,0:T(8,128)(2,1)S(1)}, bf16[1568,128]{1,0:T(8,128)(2,1)S(1)}, u32[]{:S(2)}, u32[]{:S(2)}) collective-permute-start(bf16[1568,128]{1,0:T(8,128)(2,1)S(1)} %pad_maximum_fusion.11), channel_id=1, source_target_pairs={{0,24},{8,0},{16,8},{24,16},{32,56},{40,32},{48,40},{56,48},{64,88... | collective-permute-start | bytes 1204232 | tf_op jit(solution)/shard_map/while/body/eval_jaxpr/ppermute | solution.py:44
  101.3 9.1 %attend_stage.13 = (f32[4,1,512]{2,1,0:T(1,128)S(1)}, f32[4,1,512]{2,1,0:T(1,128)S(1)}, f32[512,512]{1,0:T(8,128)}) custom-call(s32[1]{0:T(128)} %bitcast.64.number, s32[23]{0:T(128)S(1)} %get-tuple-element.483.info, bf16[512,512]{1,0:T(8,128)(2,1)S(1)} %get-tuple-element.484.queries, ...), custom_call_target="tpu_custom_call", output_to_operand_aliasing={{0}: (6, {}), {1}: (7, {}), {2}: (8, {})} | custom-call | flops 4294967296 | bytes 3145728 | tf_op jit(solution)/shard_map/while/body/eval_jaxpr/attend_stage/pallas_call | solution.py:313
  110.7 3.2 %collective-permute-start.14 = (bf16[528,128]{1,0:T(8,128)(2,1)S(1)}, bf16[528,128]{1,0:T(8,128)(2,1)S(1)}, u32[]{:S(2)}, u32[]{:S(2)}) collective-permute-start(bf16[528,128]{1,0:T(8,128)(2,1)S(1)} %slice.97), channel_id=1, source_target_pairs={{0,24},{8,0},{16,8},{24,16},{32,56},{40,32},{48,40},{56,48},{64,88... | collective-permute-start | bytes 405512 | tf_op jit(solution)/shard_map/ppermute | solution.py:44
  113.9 7.0 %attend_stage.12 = (f32[4,1,512]{2,1,0:T(1,128)S(1)}, f32[4,1,512]{2,1,0:T(1,128)S(1)}, f32[512,512]{1,0:T(8,128)}) custom-call(s32[1]{0:T(128)} %constant.160.clone.1.number, s32[23]{0:T(128)S(1)} %get-tuple-element.522, bf16[512,512]{1,0:T(8,128)(2,1)S(1)} %get-tuple-element.533, ...), custom_call_target="tpu_custom_call", output_to_operand_aliasing={{0}: (5, {}), {1}: (6, {}), {2}: (7, {})} | custom-call | flops 3221225472 | bytes 3145728 | tf_op jit(solution)/shard_map/attend_stage/pallas_call | solution.py:313
  121.0 0.6 copy-done.11
  121.6 10.1 %finish.1 = (bf16[512,512]{1,0:T(8,128)(2,1)}, bf16[3,512,512]{2,1,0:T(8,128)(2,1)}, f32[4,512,512]{2,1,0:T(8,128)}) custom-call(s32[23]{0:T(128)S(1)} %get-tuple-element.522, s32[8]{0:T(128)} %pad_add_fusion.1.columns, bf16[512,512]{1,0:T(8,128)(2,1)S(1)} %get-tuple-element.533, bf16[512,128]{1,0:T(8,128)(2,1)} %copy-done.11, bf16[528,128]{1,0:T(8,128)(2,1)} %copy-done.10, ...), custom_call_target="tpu_custom_call" | custom-call | flops 2147483648 | bytes 8388608 | tf_op jit(solution)/shard_map/finish/pallas_call | solution.py:397
  131.8 0.3 collective-permute-start.15
  132.1 0.5 collective-permute-start.16
  132.6 3.9 %collective-permute-done.16 = bf16[512,512]{1,0:T(8,128)(2,1)S(1)} collective-permute-done((bf16[512,512]{1,0:T(8,128)(2,1)}, bf16[512,512]{1,0:T(8,128)(2,1)S(1)}, u32[]{:S(2)}, u32[]{:S(2)}) %collective-permute-start.16) | collective-permute-done | bytes 524320 | tf_op jit(solution)/shard_map/ppermute | solution.py:34
  136.4 1.5 fusion
  138.0 2.8 %collective-permute-start.17 = (bf16[256,512]{1,0:T(8,128)(2,1)S(1)}, bf16[256,512]{1,0:T(8,128)(2,1)S(1)}, u32[]{:S(2)}, u32[]{:S(2)}) collective-permute-start(bf16[256,512]{1,0:T(8,128)(2,1)S(1)} %get-tuple-element.383), channel_id=1, source_target_pairs={{0,2},{2,4},{4,6},{6,0},{1,3},{3,5},{5,7},{7,1},{8,10},{10,12},{12... | collective-permute-start | bytes 786440 | tf_op jit(solution)/shard_map/ppermute | solution.py:34
  140.8 5.9 %collective-permute-done.17 = bf16[256,512]{1,0:T(8,128)(2,1)S(1)} collective-permute-done((bf16[256,512]{1,0:T(8,128)(2,1)S(1)}, bf16[256,512]{1,0:T(8,128)(2,1)S(1)}, u32[]{:S(2)}, u32[]{:S(2)}) %collective-permute-start.17) | collective-permute-done | bytes 262176 | tf_op jit(solution)/shard_map/ppermute | solution.py:34
  146.7 3.4 %collective-permute-done.21 = bf16[256,512]{1,0:T(8,128)(2,1)S(1)} collective-permute-done((bf16[256,512]{1,0:T(8,128)(2,1)S(1)}, bf16[256,512]{1,0:T(8,128)(2,1)S(1)}, u32[]{:S(2)}, u32[]{:S(2)}) %collective-permute-start.21) | collective-permute-done | bytes 262176 | tf_op jit(solution)/shard_map/ppermute | solution.py:34
  150.1 1.4 fusion.8
  151.5 0.4 collective-permute-start.18
  151.9 1.7 %collective-permute-start.22 = (bf16[256,512]{1,0:T(8,128)(2,1)S(1)}, bf16[256,512]{1,0:T(8,128)(2,1)S(1)}, u32[]{:S(2)}, u32[]{:S(2)}) collective-permute-start(bf16[256,512]{1,0:T(8,128)(2,1)S(1)} %get-tuple-element.378), channel_id=1, source_target_pairs={{0,6},{2,0},{4,2},{6,4},{1,7},{3,1},{5,3},{7,5},{8,14},{10,8},{12,... | collective-permute-start | bytes 786440 | tf_op jit(solution)/shard_map/ppermute | solution.py:34
  153.6 0.2 fusion.9
  153.9 3.2 %collective-permute-start.20 = (bf16[256,512]{1,0:T(8,128)(2,1)S(1)}, bf16[256,512]{1,0:T(8,128)(2,1)S(1)}, u32[]{:S(2)}, u32[]{:S(2)}) collective-permute-start(bf16[256,512]{1,0:T(8,128)(2,1)S(1)} %get-tuple-element.380), channel_id=1, source_target_pairs={{0,2},{2,4},{4,6},{6,0},{1,3},{3,5},{5,7},{7,1},{8,10},{10,12},{12... | collective-permute-start | bytes 786440 | tf_op jit(solution)/shard_map/ppermute | solution.py:34
  157.1 0.2 convert_add_fusion
  157.3 3.5 %collective-permute-done.18 = bf16[256,512]{1,0:T(8,128)(2,1)S(1)} collective-permute-done((bf16[256,512]{1,0:T(8,128)(2,1)S(1)}, bf16[256,512]{1,0:T(8,128)(2,1)S(1)}, u32[]{:S(2)}, u32[]{:S(2)}) %collective-permute-start.18) | collective-permute-done | bytes 262176 | tf_op jit(solution)/shard_map/ppermute | solution.py:34
  160.8 1.5 collective-permute-done.22
  162.3 3.7 %collective-permute-done.19 = bf16[256,512]{1,0:T(8,128)(2,1)S(1)} collective-permute-done((bf16[256,512]{1,0:T(8,128)(2,1)S(1)}, bf16[256,512]{1,0:T(8,128)(2,1)S(1)}, u32[]{:S(2)}, u32[]{:S(2)}) %collective-permute-start.19) | collective-permute-done | bytes 262176 | tf_op jit(solution)/shard_map/ppermute | solution.py:34
  165.9 0.2 fusion.6
  166.2 0.8 pad_maximum_fusion.5
  (99 shorter events, 1.9 us)
Async XLA Ops:
  1.8 17.6 %copy-start.4 = (bf16[528,512]{1,0:T(8,128)(2,1)}, bf16[528,512]{1,0:T(8,128)(2,1)S(1)}, u32[]{:S(2)}) copy-start(bf16[528,512]{1,0:T(8,128)(2,1)S(1)} %pad_maximum_fusion.3.x0) | copy-start | bytes 1622020
  1.8 12.0 %collective-permute-start.5 = (bf16[528,512]{1,0:T(8,128)(2,1)S(1)}, bf16[528,512]{1,0:T(8,128)(2,1)S(1)}, u32[]{:S(2)}, u32[]{:S(2)}) collective-permute-start(bf16[528,512]{1,0:T(8,128)(2,1)S(1)} %pad_maximum_fusion.3.x0), channel_id=1, source_target_pairs={{0,1},{1,0},{2,3},{3,2},{4,5},{5,4},{6,7},{7,6},{8,9},{9,8},{10,11... | collective-permute-start | bytes 1622024 | tf_op jit(solution)/shard_map/ppermute | solution.py:34
  1.9 15.9 %collective-permute-start.4 = (bf16[528,512]{1,0:T(8,128)(2,1)S(1)}, bf16[528,512]{1,0:T(8,128)(2,1)S(1)}, u32[]{:S(2)}, u32[]{:S(2)}) collective-permute-start(bf16[528,512]{1,0:T(8,128)(2,1)S(1)} %pad_maximum_fusion.3.x0), channel_id=1, source_target_pairs={{0,6},{2,0},{4,2},{6,4},{1,7},{3,1},{5,3},{7,5},{8,14},{10,8},{12,... | collective-permute-start | bytes 1622024 | tf_op jit(solution)/shard_map/ppermute | solution.py:34
  2.8 15.0 %collective-permute-start.3 = (bf16[528,512]{1,0:T(8,128)(2,1)S(1)}, bf16[528,512]{1,0:T(8,128)(2,1)S(1)}, u32[]{:S(2)}, u32[]{:S(2)}) collective-permute-start(bf16[528,512]{1,0:T(8,128)(2,1)S(1)} %pad_maximum_fusion.3.x0), channel_id=1, source_target_pairs={{0,2},{2,4},{4,6},{6,0},{1,3},{3,5},{5,7},{7,1},{8,10},{10,12},{12... | collective-permute-start | bytes 1622024 | tf_op jit(solution)/shard_map/ppermute | solution.py:34
  13.8 5.8 %copy-start.8 = (bf16[528,512]{1,0:T(8,128)(2,1)}, bf16[528,512]{1,0:T(8,128)(2,1)S(1)}, u32[]{:S(2)}) copy-start(bf16[528,512]{1,0:T(8,128)(2,1)S(1)} %collective-permute-done.5.x1) | copy-start | bytes 1622020
  17.8 1.9 %copy-start.2 = (bf16[528,512]{1,0:T(8,128)(2,1)}, bf16[528,512]{1,0:T(8,128)(2,1)S(1)}, u32[]{:S(2)}) copy-start(bf16[528,512]{1,0:T(8,128)(2,1)S(1)} %collective-permute-done.4.m0) | copy-start | bytes 1622020
  17.8 1.9 %copy-start.3 = (bf16[528,512]{1,0:T(8,128)(2,1)}, bf16[528,512]{1,0:T(8,128)(2,1)S(1)}, u32[]{:S(2)}) copy-start(bf16[528,512]{1,0:T(8,128)(2,1)S(1)} %collective-permute-done.3.p0) | copy-start | bytes 1622020
  19.4 12.5 %collective-permute-start.8 = (bf16[1056,512]{1,0:T(8,128)(2,1)S(1)}, bf16[1056,512]{1,0:T(8,128)(2,1)S(1)}, u32[]{:S(2)}, u32[]{:S(2)}) collective-permute-start(bf16[1056,512]{1,0:T(8,128)(2,1)S(1)} %pad_maximum_fusion.2), channel_id=1, source_target_pairs={{0,1},{1,0},{2,3},{3,2},{4,5},{5,4},{6,7},{7,6},{8,9},{9,8},{10,11... | collective-permute-start | bytes 3244040 | tf_op jit(solution)/shard_map/ppermute | solution.py:34
  19.5 10.3 %collective-permute-start.7 = (bf16[272,512]{1,0:T(8,128)(2,1)S(1)}, bf16[272,512]{1,0:T(8,128)(2,1)S(1)}, u32[]{:S(2)}, u32[]{:S(2)}) collective-permute-start(bf16[272,512]{1,0:T(8,128)(2,1)S(1)} %slice.95), channel_id=1, source_target_pairs={{0,6},{2,0},{4,2},{6,4},{1,7},{3,1},{5,3},{7,5},{8,14},{10,8},{12,... | collective-permute-start | bytes 835592 | tf_op jit(solution)/shard_map/ppermute | solution.py:34
  19.6 9.2 %collective-permute-start.6 = (bf16[256,512]{1,0:T(8,128)(2,1)S(1)}, bf16[256,512]{1,0:T(8,128)(2,1)S(1)}, u32[]{:S(2)}, u32[]{:S(2)}) collective-permute-start(bf16[256,512]{1,0:T(8,128)(2,1)S(1)} %slice.94), channel_id=1, source_target_pairs={{0,2},{2,4},{4,6},{6,0},{1,3},{3,5},{5,7},{7,1},{8,10},{10,12},{12... | collective-permute-start | bytes 786440 | tf_op jit(solution)/shard_map/ppermute | solution.py:34
  28.9 3.0 %copy-start.6 = (bf16[256,512]{1,0:T(8,128)(2,1)}, bf16[256,512]{1,0:T(8,128)(2,1)S(1)}, u32[]{:S(2)}) copy-start(bf16[256,512]{1,0:T(8,128)(2,1)S(1)} %collective-permute-done.6.q0) | copy-start | bytes 786436
  29.8 2.1 %copy-start.5 = (bf16[272,512]{1,0:T(8,128)(2,1)}, bf16[272,512]{1,0:T(8,128)(2,1)S(1)}, u32[]{:S(2)}) copy-start(bf16[272,512]{1,0:T(8,128)(2,1)S(1)} %collective-permute-done.7.r0) | copy-start | bytes 835588
  29.9 2.0 %collective-permute-start.9 = (bf16[528,512]{1,0:T(8,128)(2,1)S(1)}, bf16[528,512]{1,0:T(8,128)(2,1)S(1)}, u32[]{:S(2)}, u32[]{:S(2)}) collective-permute-start(bf16[528,512]{1,0:T(8,128)(2,1)S(1)} %pad_maximum_fusion.4), channel_id=1, source_target_pairs={{0,1},{1,0},{2,3},{3,2},{4,5},{5,4},{6,7},{7,6},{8,9},{9,8},{10,11... | collective-permute-start | bytes 1622024 | tf_op jit(solution)/shard_map/ppermute | solution.py:34
  31.9 0.8 copy-start.9
  32.7 1.0 copy-start.7
  43.3 9.4 %collective-permute-start.11 = (bf16[1040,128]{1,0:T(8,128)(2,1)}, bf16[1040,128]{1,0:T(8,128)(2,1)S(1)}, u32[]{:S(2)}, u32[]{:S(2)}) collective-permute-start(bf16[1040,128]{1,0:T(8,128)(2,1)} %get-tuple-element.335.message), channel_id=1, source_target_pairs={{0,24},{8,0},{16,8},{24,16},{32,56},{40,32},{48,40},{56,48},{64,88... | collective-permute-start | bytes 798728 | tf_op jit(solution)/shard_map/ppermute | solution.py:44
  46.4 9.6 %collective-permute-start.10 = (bf16[1040,128]{1,0:T(8,128)(2,1)}, bf16[1040,128]{1,0:T(8,128)(2,1)S(1)}, u32[]{:S(2)}, u32[]{:S(2)}) collective-permute-start(bf16[1040,128]{1,0:T(8,128)(2,1)} %get-tuple-element.335.message), channel_id=1, source_target_pairs={{0,8},{8,16},{16,24},{24,0},{32,40},{40,48},{48,56},{56,32},{64,72... | collective-permute-start | bytes 798728 | tf_op jit(solution)/shard_map/ppermute | solution.py:44
  46.4 9.6 %collective-permute-start.12 = (bf16[1040,128]{1,0:T(8,128)(2,1)}, bf16[1040,128]{1,0:T(8,128)(2,1)S(1)}, u32[]{:S(2)}, u32[]{:S(2)}) collective-permute-start(bf16[1040,128]{1,0:T(8,128)(2,1)} %get-tuple-element.335.message), channel_id=1, source_target_pairs={{0,32},{8,40},{16,48},{24,56},{32,64},{40,72},{48,80},{56,88},{64,... | collective-permute-start | bytes 798728 | tf_op jit(solution)/shard_map/ppermute | solution.py:38
  56.1 4.6 %copy-start = (bf16[1040,128]{1,0:T(8,128)(2,1)}, bf16[1040,128]{1,0:T(8,128)(2,1)S(1)}, u32[]{:S(2)}) copy-start(bf16[1040,128]{1,0:T(8,128)(2,1)S(1)} %copy.25.refs_2_) | copy-start | bytes 798724 | tf_op jit(solution)/shard_map/while
  56.1 12.3 %collective-permute-start.2 = (bf16[1040,128]{1,0:T(8,128)(2,1)S(1)}, bf16[1040,128]{1,0:T(8,128)(2,1)S(1)}, u32[]{:S(2)}, u32[]{:S(2)}) collective-permute-start(bf16[1040,128]{1,0:T(8,128)(2,1)S(1)} %copy.25.refs_2_), channel_id=1, source_target_pairs={{0,32},{8,40},{16,48},{24,56},{32,64},{40,72},{48,80},{56,88},{64,... | collective-permute-start | bytes 798728 | tf_op jit(solution)/shard_map/while/body/eval_jaxpr/ppermute | solution.py:38
  57.2 11.1 %collective-permute-start = (bf16[1552,128]{1,0:T(8,128)(2,1)S(1)}, bf16[1552,128]{1,0:T(8,128)(2,1)S(1)}, u32[]{:S(2)}, u32[]{:S(2)}) collective-permute-start(bf16[1552,128]{1,0:T(8,128)(2,1)S(1)} %pad_maximum_fusion.10), channel_id=1, source_target_pairs={{0,8},{8,16},{16,24},{24,0},{32,40},{40,48},{48,56},{56,32},{64,72... | collective-permute-start | bytes 1191944 | tf_op jit(solution)/shard_map/while/body/eval_jaxpr/ppermute | solution.py:44
  57.4 11.0 %collective-permute-start.1 = (bf16[1568,128]{1,0:T(8,128)(2,1)S(1)}, bf16[1568,128]{1,0:T(8,128)(2,1)S(1)}, u32[]{:S(2)}, u32[]{:S(2)}) collective-permute-start(bf16[1568,128]{1,0:T(8,128)(2,1)S(1)} %pad_maximum_fusion.11), channel_id=1, source_target_pairs={{0,24},{8,0},{16,8},{24,16},{32,56},{40,32},{48,40},{56,48},{64,88... | collective-permute-start | bytes 1204232 | tf_op jit(solution)/shard_map/while/body/eval_jaxpr/ppermute | solution.py:44
  68.5 4.6 %copy-start = (bf16[1040,128]{1,0:T(8,128)(2,1)}, bf16[1040,128]{1,0:T(8,128)(2,1)S(1)}, u32[]{:S(2)}) copy-start(bf16[1040,128]{1,0:T(8,128)(2,1)S(1)} %copy.25.refs_2_) | copy-start | bytes 798724 | tf_op jit(solution)/shard_map/while
  68.5 13.3 %collective-permute-start.2 = (bf16[1040,128]{1,0:T(8,128)(2,1)S(1)}, bf16[1040,128]{1,0:T(8,128)(2,1)S(1)}, u32[]{:S(2)}, u32[]{:S(2)}) collective-permute-start(bf16[1040,128]{1,0:T(8,128)(2,1)S(1)} %copy.25.refs_2_), channel_id=1, source_target_pairs={{0,32},{8,40},{16,48},{24,56},{32,64},{40,72},{48,80},{56,88},{64,... | collective-permute-start | bytes 798728 | tf_op jit(solution)/shard_map/while/body/eval_jaxpr/ppermute | solution.py:38
  69.6 12.1 %collective-permute-start = (bf16[1552,128]{1,0:T(8,128)(2,1)S(1)}, bf16[1552,128]{1,0:T(8,128)(2,1)S(1)}, u32[]{:S(2)}, u32[]{:S(2)}) collective-permute-start(bf16[1552,128]{1,0:T(8,128)(2,1)S(1)} %pad_maximum_fusion.10), channel_id=1, source_target_pairs={{0,8},{8,16},{16,24},{24,0},{32,40},{40,48},{48,56},{56,32},{64,72... | collective-permute-start | bytes 1191944 | tf_op jit(solution)/shard_map/while/body/eval_jaxpr/ppermute | solution.py:44
  69.8 12.0 %collective-permute-start.1 = (bf16[1568,128]{1,0:T(8,128)(2,1)S(1)}, bf16[1568,128]{1,0:T(8,128)(2,1)S(1)}, u32[]{:S(2)}, u32[]{:S(2)}) collective-permute-start(bf16[1568,128]{1,0:T(8,128)(2,1)S(1)} %pad_maximum_fusion.11), channel_id=1, source_target_pairs={{0,24},{8,0},{16,8},{24,16},{32,56},{40,32},{48,40},{56,48},{64,88... | collective-permute-start | bytes 1204232 | tf_op jit(solution)/shard_map/while/body/eval_jaxpr/ppermute | solution.py:44
  81.9 4.7 %copy-start = (bf16[1040,128]{1,0:T(8,128)(2,1)}, bf16[1040,128]{1,0:T(8,128)(2,1)S(1)}, u32[]{:S(2)}) copy-start(bf16[1040,128]{1,0:T(8,128)(2,1)S(1)} %copy.25.refs_2_) | copy-start | bytes 798724 | tf_op jit(solution)/shard_map/while
  81.9 15.8 %collective-permute-start.2 = (bf16[1040,128]{1,0:T(8,128)(2,1)S(1)}, bf16[1040,128]{1,0:T(8,128)(2,1)S(1)}, u32[]{:S(2)}, u32[]{:S(2)}) collective-permute-start(bf16[1040,128]{1,0:T(8,128)(2,1)S(1)} %copy.25.refs_2_), channel_id=1, source_target_pairs={{0,32},{8,40},{16,48},{24,56},{32,64},{40,72},{48,80},{56,88},{64,... | collective-permute-start | bytes 798728 | tf_op jit(solution)/shard_map/while/body/eval_jaxpr/ppermute | solution.py:38
  82.0 15.6 %collective-permute-start = (bf16[1552,128]{1,0:T(8,128)(2,1)S(1)}, bf16[1552,128]{1,0:T(8,128)(2,1)S(1)}, u32[]{:S(2)}, u32[]{:S(2)}) collective-permute-start(bf16[1552,128]{1,0:T(8,128)(2,1)S(1)} %pad_maximum_fusion.10), channel_id=1, source_target_pairs={{0,8},{8,16},{16,24},{24,0},{32,40},{40,48},{48,56},{56,32},{64,72... | collective-permute-start | bytes 1191944 | tf_op jit(solution)/shard_map/while/body/eval_jaxpr/ppermute | solution.py:44
  82.2 15.4 %collective-permute-start.1 = (bf16[1568,128]{1,0:T(8,128)(2,1)S(1)}, bf16[1568,128]{1,0:T(8,128)(2,1)S(1)}, u32[]{:S(2)}, u32[]{:S(2)}) collective-permute-start(bf16[1568,128]{1,0:T(8,128)(2,1)S(1)} %pad_maximum_fusion.11), channel_id=1, source_target_pairs={{0,24},{8,0},{16,8},{24,16},{32,56},{40,32},{48,40},{56,48},{64,88... | collective-permute-start | bytes 1204232 | tf_op jit(solution)/shard_map/while/body/eval_jaxpr/ppermute | solution.py:44
  97.7 3.6 %copy-start = (bf16[1040,128]{1,0:T(8,128)(2,1)}, bf16[1040,128]{1,0:T(8,128)(2,1)S(1)}, u32[]{:S(2)}) copy-start(bf16[1040,128]{1,0:T(8,128)(2,1)S(1)} %copy.25.refs_2_) | copy-start | bytes 798724 | tf_op jit(solution)/shard_map/while
  97.8 12.8 %collective-permute-start.2 = (bf16[1040,128]{1,0:T(8,128)(2,1)S(1)}, bf16[1040,128]{1,0:T(8,128)(2,1)S(1)}, u32[]{:S(2)}, u32[]{:S(2)}) collective-permute-start(bf16[1040,128]{1,0:T(8,128)(2,1)S(1)} %copy.25.refs_2_), channel_id=1, source_target_pairs={{0,32},{8,40},{16,48},{24,56},{32,64},{40,72},{48,80},{56,88},{64,... | collective-permute-start | bytes 798728 | tf_op jit(solution)/shard_map/while/body/eval_jaxpr/ppermute | solution.py:38
  97.9 12.5 %collective-permute-start = (bf16[1552,128]{1,0:T(8,128)(2,1)S(1)}, bf16[1552,128]{1,0:T(8,128)(2,1)S(1)}, u32[]{:S(2)}, u32[]{:S(2)}) collective-permute-start(bf16[1552,128]{1,0:T(8,128)(2,1)S(1)} %pad_maximum_fusion.10), channel_id=1, source_target_pairs={{0,8},{8,16},{16,24},{24,0},{32,40},{40,48},{48,56},{56,32},{64,72... | collective-permute-start | bytes 1191944 | tf_op jit(solution)/shard_map/while/body/eval_jaxpr/ppermute | solution.py:44
  98.0 12.4 %collective-permute-start.1 = (bf16[1568,128]{1,0:T(8,128)(2,1)S(1)}, bf16[1568,128]{1,0:T(8,128)(2,1)S(1)}, u32[]{:S(2)}, u32[]{:S(2)}) collective-permute-start(bf16[1568,128]{1,0:T(8,128)(2,1)S(1)} %pad_maximum_fusion.11), channel_id=1, source_target_pairs={{0,24},{8,0},{16,8},{24,16},{32,56},{40,32},{48,40},{56,48},{64,88... | collective-permute-start | bytes 1204232 | tf_op jit(solution)/shard_map/while/body/eval_jaxpr/ppermute | solution.py:44
  110.6 10.3 %collective-permute-start.13 = (bf16[512,128]{1,0:T(8,128)(2,1)S(1)}, bf16[512,128]{1,0:T(8,128)(2,1)S(1)}, u32[]{:S(2)}, u32[]{:S(2)}) collective-permute-start(bf16[512,128]{1,0:T(8,128)(2,1)S(1)} %slice.96), channel_id=1, source_target_pairs={{0,8},{8,16},{16,24},{24,0},{32,40},{40,48},{48,56},{56,32},{64,72... | collective-permute-start | bytes 393224 | tf_op jit(solution)/shard_map/ppermute | solution.py:44
  110.7 10.3 %collective-permute-start.14 = (bf16[528,128]{1,0:T(8,128)(2,1)S(1)}, bf16[528,128]{1,0:T(8,128)(2,1)S(1)}, u32[]{:S(2)}, u32[]{:S(2)}) collective-permute-start(bf16[528,128]{1,0:T(8,128)(2,1)S(1)} %slice.97), channel_id=1, source_target_pairs={{0,24},{8,0},{16,8},{24,16},{32,56},{40,32},{48,40},{56,48},{64,88... | collective-permute-start | bytes 405512 | tf_op jit(solution)/shard_map/ppermute | solution.py:44
  120.9 0.6 copy-start.11
  120.9 0.7 copy-start.10
  131.8 18.4 %collective-permute-start.15 = (bf16[3,512,512]{2,1,0:T(8,128)(2,1)}, bf16[3,512,512]{2,1,0:T(8,128)(2,1)S(1)}, u32[]{:S(2)}, u32[]{:S(2)}) collective-permute-start(bf16[3,512,512]{2,1,0:T(8,128)(2,1)} %get-tuple-element.353), channel_id=1, source_target_pairs={{0,1},{1,0},{2,3},{3,2},{4,5},{5,4},{6,7},{7,6},{8,9},{9,8},{10,11... | collective-permute-start | bytes 4718600 | tf_op jit(solution)/shard_map/ppermute | solution.py:34
  132.1 4.4 %collective-permute-start.16 = (bf16[512,512]{1,0:T(8,128)(2,1)}, bf16[512,512]{1,0:T(8,128)(2,1)S(1)}, u32[]{:S(2)}, u32[]{:S(2)}) collective-permute-start(bf16[512,512]{1,0:T(8,128)(2,1)} %get-tuple-element.354), channel_id=1, source_target_pairs={{0,1},{1,0},{2,3},{3,2},{4,5},{5,4},{6,7},{7,6},{8,9},{9,8},{10,11... | collective-permute-start | bytes 1572872 | tf_op jit(solution)/shard_map/ppermute | solution.py:34
  136.4 17.2 %copy-start.1 = (f32[4,512,512]{2,1,0:T(8,128)S(1)}, f32[4,512,512]{2,1,0:T(8,128)}, u32[]{:S(2)}) copy-start(f32[4,512,512]{2,1,0:T(8,128)} %get-tuple-element.352) | copy-start | bytes 12582916
  138.0 8.7 %collective-permute-start.17 = (bf16[256,512]{1,0:T(8,128)(2,1)S(1)}, bf16[256,512]{1,0:T(8,128)(2,1)S(1)}, u32[]{:S(2)}, u32[]{:S(2)}) collective-permute-start(bf16[256,512]{1,0:T(8,128)(2,1)S(1)} %get-tuple-element.383), channel_id=1, source_target_pairs={{0,2},{2,4},{4,6},{6,0},{1,3},{3,5},{5,7},{7,1},{8,10},{10,12},{12... | collective-permute-start | bytes 786440 | tf_op jit(solution)/shard_map/ppermute | solution.py:34
  140.8 9.3 %collective-permute-start.21 = (bf16[256,512]{1,0:T(8,128)(2,1)S(1)}, bf16[256,512]{1,0:T(8,128)(2,1)S(1)}, u32[]{:S(2)}, u32[]{:S(2)}) collective-permute-start(bf16[256,512]{1,0:T(8,128)(2,1)S(1)} %get-tuple-element.384), channel_id=1, source_target_pairs={{0,6},{2,0},{4,2},{6,4},{1,7},{3,1},{5,3},{7,5},{8,14},{10,8},{12,... | collective-permute-start | bytes 786440 | tf_op jit(solution)/shard_map/ppermute | solution.py:34
  151.5 9.3 %collective-permute-start.18 = (bf16[256,512]{1,0:T(8,128)(2,1)S(1)}, bf16[256,512]{1,0:T(8,128)(2,1)S(1)}, u32[]{:S(2)}, u32[]{:S(2)}) collective-permute-start(bf16[256,512]{1,0:T(8,128)(2,1)S(1)} %get-tuple-element.377), channel_id=1, source_target_pairs={{0,2},{2,4},{4,6},{6,0},{1,3},{3,5},{5,7},{7,1},{8,10},{10,12},{12... | collective-permute-start | bytes 786440 | tf_op jit(solution)/shard_map/ppermute | solution.py:34
  151.9 10.4 %collective-permute-start.22 = (bf16[256,512]{1,0:T(8,128)(2,1)S(1)}, bf16[256,512]{1,0:T(8,128)(2,1)S(1)}, u32[]{:S(2)}, u32[]{:S(2)}) collective-permute-start(bf16[256,512]{1,0:T(8,128)(2,1)S(1)} %get-tuple-element.378), channel_id=1, source_target_pairs={{0,6},{2,0},{4,2},{6,4},{1,7},{3,1},{5,3},{7,5},{8,14},{10,8},{12,... | collective-permute-start | bytes 786440 | tf_op jit(solution)/shard_map/ppermute | solution.py:34
  153.8 12.1 %collective-permute-start.19 = (bf16[256,512]{1,0:T(8,128)(2,1)S(1)}, bf16[256,512]{1,0:T(8,128)(2,1)S(1)}, u32[]{:S(2)}, u32[]{:S(2)}) collective-permute-start(bf16[256,512]{1,0:T(8,128)(2,1)S(1)} %get-tuple-element.379), channel_id=1, source_target_pairs={{0,6},{2,0},{4,2},{6,4},{1,7},{3,1},{5,3},{7,5},{8,14},{10,8},{12,... | collective-permute-start | bytes 786440 | tf_op jit(solution)/shard_map/ppermute | solution.py:34
  153.9 12.0 %collective-permute-start.20 = (bf16[256,512]{1,0:T(8,128)(2,1)S(1)}, bf16[256,512]{1,0:T(8,128)(2,1)S(1)}, u32[]{:S(2)}, u32[]{:S(2)}) collective-permute-start(bf16[256,512]{1,0:T(8,128)(2,1)S(1)} %get-tuple-element.380), channel_id=1, source_target_pairs={{0,2},{2,4},{4,6},{6,0},{1,3},{3,5},{5,7},{7,1},{8,10},{10,12},{12... | collective-permute-start | bytes 786440 | tf_op jit(solution)/shard_map/ppermute | solution.py:34
